TPU v7x, 256 devices: a whole 4x4x8 slice. The times are simulated.
256 devices in a mesh: row: 8 (over x, core), col: 32 (over z, y).
Axes of the slice: x: 4, y: 4, z: 8, core: 2. Of those that a mesh axis runs over, the one named last changes fastest.
Arguments:
- x_rows: float32 [16, 32768], P(None, ('row', 'col')), may hold values from -6 to 6
- alpha_rows: float32 [32768], P(('row', 'col')), may hold values from -0.5 to 1.5
- x_cols: float32 [16, 32768], P(None, ('col', 'row')), may hold values from -6 to 6
- alpha_cols: float32 [32768], P(('col', 'row')), may hold values from -0.0018310547 to 0.005493164
- lengthscale: float32 [16], replicated, may hold values from 1.2 to 2.5
Outputs:
- row_terms: float32 [16, 32768], P(None, ('row', 'col'))
- kernel_alpha: float32 [32768], P(('row', 'col'))
- grad: float32 [16], replicated
All inputs are finite; a program needn't handle non-finite values.
Results may differ from a plain program's by a relative error of at most 0.00021.
Values sent between devices are 32-bit elements; how exact they have to be, the bound alone decides.
No kernel may reach another device: no remote copies, remote signals or barrier semaphores. Data moves between devices by JAX's collectives and lax.ppermute only.
A program may use at most 64 MiB of HBM per device.

v0:
```python
import jax
import jax.numpy as jnp
from jax import lax
from jax.sharding import Mesh
from jax.sharding import PartitionSpec as P

COL = ("col_0", "col_1")
ROW = ("row_0", "row_1")
ROW_COL = ("row_0", "row_1", "col_0", "col_1")
COL_ROW = ("col_0", "col_1", "row_0", "row_1")


def copy_for_each(x, axis):
    copies = jnp.broadcast_to(x, (lax.axis_size(axis), *x.shape))
    return lax.all_to_all(copies, axis, split_axis=0, concat_axis=0, tiled=True)


def joined_along(blocks, dim):
    shape = list(blocks.shape[1:])
    shape[dim] *= blocks.shape[0]
    return jnp.moveaxis(blocks, 0, dim).reshape(shape)


def gathered_copies(x, axis, dim):
    blocks = copy_for_each(x, axis)
    return joined_along(blocks, dim)


def gathered_by_axis(x, axes, dim):
    result = x
    for number in range(len(axes) - 1, -1, -1):
        result = lax.all_gather(result, axes[number], axis=dim, tiled=True)
    return result


def cut_along(x, dim, devices):
    before, after = (x.shape[:dim], x.shape[dim + 1 :])
    return jnp.moveaxis(x.reshape(*before, devices, -1, *after), dim, 0)


def sent_and_summed(x, axis, dim):
    blocks = cut_along(x, dim, lax.axis_size(axis))
    arrived = lax.all_to_all(blocks, axis, split_axis=0, concat_axis=0, tiled=True)
    return arrived.sum(axis=0)


def one_axis_at_a_time(x, axes):
    for axis in axes:
        x = lax.psum(x, axis)
    return x


def fold_terms(partials, row_scaled, row_alpha):
    dims = row_scaled.shape[0]
    weight_sum = partials[0]
    first_moment = partials[1 : 1 + dims]
    second_moment = partials[1 + dims :]
    terms = (
        0.5
        * row_alpha[None, :]
        * (
            row_scaled * row_scaled * weight_sum[None, :]
            - 2.0 * row_scaled * first_moment
            + second_moment
        )
    )
    return (terms, weight_sum)


def on_device(x_rows, alpha_rows, x_cols, alpha_cols, lengthscale):
    dims = x_rows.shape[0]
    inverse_scale = 1.0 / lengthscale
    own_scaled = x_rows * inverse_scale[:, None]
    own_rows = jnp.concatenate([own_scaled, alpha_rows[None, :]], 0)
    gathered = gathered_copies(own_rows, COL, 1)
    row_scaled = gathered[:dims]
    row_alpha = gathered[dims]
    row_count = row_scaled.shape[1]
    block_rows = min(512, row_count)
    block_count = row_count // block_rows
    row_norms = jnp.sum(row_scaled * row_scaled, 0)
    own_cols = jnp.concatenate([x_cols * inverse_scale[:, None], alpha_cols[None, :]], 0)
    empty = jnp.zeros((2 * dims + 1, row_count), jnp.float32)
    shard_piece = gathered_by_axis(own_cols, ROW, 1)
    col_scaled = shard_piece[:dims]
    col_alpha = shard_piece[dims]
    col_norms = jnp.sum(col_scaled * col_scaled, 0)
    values = jnp.concatenate(
        [
            col_alpha[None, :],
            col_alpha[None, :] * col_scaled,
            col_alpha[None, :] * col_scaled * col_scaled,
        ],
        0,
    )

    def add_block(block_index, carried):
        offset = block_index * block_rows
        row_block = lax.dynamic_slice_in_dim(row_scaled, offset, block_rows, 1)
        block_norms = lax.dynamic_slice_in_dim(row_norms, offset, block_rows, 0)
        cross = lax.dot_general(
            row_block,
            col_scaled,
            (((0,), (0,)), ((), ())),
            precision=lax.Precision.HIGHEST,
            preferred_element_type=jnp.float32,
        )
        kernel = jnp.exp(-0.5 * (block_norms[:, None] + col_norms[None, :] - 2.0 * cross))
        contrib = lax.dot_general(
            values,
            kernel,
            (((1,), (1,)), ((), ())),
            precision=lax.Precision.HIGHEST,
            preferred_element_type=jnp.float32,
        )
        earlier = lax.dynamic_slice_in_dim(carried, offset, block_rows, 1)
        return lax.dynamic_update_slice_in_dim(carried, earlier + contrib, offset, 1)

    partials = lax.fori_loop(0, block_count, add_block, empty)
    tile_terms, tile_sum = fold_terms(partials, row_scaled, row_alpha)
    stacked = jnp.concatenate([tile_terms, tile_sum[None, :]], 0)
    summed = sent_and_summed(stacked, COL, 1)
    row_terms = summed[:dims]
    kernel_alpha = summed[dims]
    total_rows = row_count * lax.axis_size(ROW)
    grad = one_axis_at_a_time(jnp.sum(tile_terms, 1), ROW_COL) / total_rows
    return (row_terms, kernel_alpha, grad)


def solution(mesh):
    finer = Mesh(mesh.devices.reshape(4, 2, 8, 4), ("row_0", "row_1", "col_0", "col_1"))
    in_specs = (P(None, ROW_COL), P(ROW_COL), P(None, COL_ROW), P(COL_ROW), P())
    out_specs = (P(None, ROW_COL), P(ROW_COL), P())
    return jax.shard_map(
        on_device, mesh=finer, in_specs=in_specs, out_specs=out_specs, check_vma=False
    )
```

profile of v0, /device:TPU:32, one launch (start us, length us, event | category | flops | bytes accessed | tf_op | source)
XLA Modules:
  0.0 117.0 jit_solution(7533206335803984260)
XLA Ops:
  3.5 11.4 %all-to-all-start = ((f32[32,17,128]{2,1,0:T(8,128)}), f32[32,17,128]{2,1,0:T(8,128)S(1)}, u32[]{:S(2)}, u32[]{:S(2)}) async-start(f32[32,17,128]{2,1,0:T(8,128)} %broadcast_in_dim.21), calls=%async_computation | async-start | bytes 786432 | tf_op jit(solution)/shard_map/all_to_all | solution.py:15
  17.3 12.3 %all_gather.7 = f32[17,1024]{1,0:T(8,128)S(1)} all-gather(f32[17,256]{1,0:T(8,128)S(1)} %all_gather.6), channel_id=1, replica_groups=mesh['row_0'=4,'row_1'=2,'col_0'=8,'col_1'=4] {'row_0'}, dimensions={1}, use_global_device_ids=true | all-gather | bytes 87040 | tf_op jit(solution)/shard_map/all_gather | solution.py:32
  29.8 35.8 %while.13 = (s32[]{:T(128)}, f32[33,4096]{1,0:T(8,128)S(1)}, f32[4096]{0:T(1024)S(1)}, f32[1024]{0:T(1024)S(1)}, f32[16,4096]{1,0:T(8,128)S(1)}, /*index=5*/f32[...) while((s32[]{:T(128)}, f32[33,4096]{1,0:T(8,128)S(1)}, ...), condition=%wide.region_3.0_spmd, body=%wide.region_2.0_spmd.sunk | while | flops 310395392 | bytes 4630695 | solution.py:119
  29.9 1.8 %fusion.38 = f32[512,1024]{1,0:T(8,128)S(1)} fusion(f32[16,1024]{1,0:T(8,128)S(1)} %get-tuple-element.222, f32[16,4096]{1,0:T(8,128)S(1)} %get-tuple-element.221, s32[]{:T(128)S(6)} %select_n.11), kind=kOutput, calls=%fused_computation.13.clone.1 | convolution fusion | flops 100663296 | bytes 2195460 | tf_op jit(solution)/shard_map/while/body/eval_jaxpr/dot_general | solution.py:101
  31.8 2.5 %fusion.39 = f32[33,4096]{1,0:T(8,128)S(1)} fusion(f32[33,4096]{1,0:T(8,128)S(1)} %get-tuple-element.207, s32[]{:T(128)S(6)} %select_n.11, f32[33,1024]{1,0:T(8,128)S(1)} %get-tuple-element.223, f32[512,1024]{1,0:T(8,128)S(1)} %fusion.38, f32[1024]{0:T(1024)S(1)} %get-tuple-element.220, f32[512]{0:T(512)S(1)} %dynamic_slice.29), kind=kOutput, calls=%fused_computation.8.clone.1 | convolution fusion | flops 209732096 | bytes 2430980 | tf_op jit(solution)/shard_map/while/body/eval_jaxpr/dot_general | solution.py:109
  34.4 1.8 %fusion.38 = f32[512,1024]{1,0:T(8,128)S(1)} fusion(f32[16,1024]{1,0:T(8,128)S(1)} %get-tuple-element.222, f32[16,4096]{1,0:T(8,128)S(1)} %get-tuple-element.221, s32[]{:T(128)S(6)} %select_n.11), kind=kOutput, calls=%fused_computation.13.clone.1 | convolution fusion | flops 100663296 | bytes 2195460 | tf_op jit(solution)/shard_map/while/body/eval_jaxpr/dot_general | solution.py:101
  36.3 2.5 %fusion.39 = f32[33,4096]{1,0:T(8,128)S(1)} fusion(f32[33,4096]{1,0:T(8,128)S(1)} %get-tuple-element.207, s32[]{:T(128)S(6)} %select_n.11, f32[33,1024]{1,0:T(8,128)S(1)} %get-tuple-element.223, f32[512,1024]{1,0:T(8,128)S(1)} %fusion.38, f32[1024]{0:T(1024)S(1)} %get-tuple-element.220, f32[512]{0:T(512)S(1)} %dynamic_slice.29), kind=kOutput, calls=%fused_computation.8.clone.1 | convolution fusion | flops 209732096 | bytes 2430980 | tf_op jit(solution)/shard_map/while/body/eval_jaxpr/dot_general | solution.py:109
  38.9 1.8 %fusion.38 = f32[512,1024]{1,0:T(8,128)S(1)} fusion(f32[16,1024]{1,0:T(8,128)S(1)} %get-tuple-element.222, f32[16,4096]{1,0:T(8,128)S(1)} %get-tuple-element.221, s32[]{:T(128)S(6)} %select_n.11), kind=kOutput, calls=%fused_computation.13.clone.1 | convolution fusion | flops 100663296 | bytes 2195460 | tf_op jit(solution)/shard_map/while/body/eval_jaxpr/dot_general | solution.py:101
  40.7 2.5 %fusion.39 = f32[33,4096]{1,0:T(8,128)S(1)} fusion(f32[33,4096]{1,0:T(8,128)S(1)} %get-tuple-element.207, s32[]{:T(128)S(6)} %select_n.11, f32[33,1024]{1,0:T(8,128)S(1)} %get-tuple-element.223, f32[512,1024]{1,0:T(8,128)S(1)} %fusion.38, f32[1024]{0:T(1024)S(1)} %get-tuple-element.220, f32[512]{0:T(512)S(1)} %dynamic_slice.29), kind=kOutput, calls=%fused_computation.8.clone.1 | convolution fusion | flops 209732096 | bytes 2430980 | tf_op jit(solution)/shard_map/while/body/eval_jaxpr/dot_general | solution.py:109
  43.4 1.8 %fusion.38 = f32[512,1024]{1,0:T(8,128)S(1)} fusion(f32[16,1024]{1,0:T(8,128)S(1)} %get-tuple-element.222, f32[16,4096]{1,0:T(8,128)S(1)} %get-tuple-element.221, s32[]{:T(128)S(6)} %select_n.11), kind=kOutput, calls=%fused_computation.13.clone.1 | convolution fusion | flops 100663296 | bytes 2195460 | tf_op jit(solution)/shard_map/while/body/eval_jaxpr/dot_general | solution.py:101
  45.2 2.5 %fusion.39 = f32[33,4096]{1,0:T(8,128)S(1)} fusion(f32[33,4096]{1,0:T(8,128)S(1)} %get-tuple-element.207, s32[]{:T(128)S(6)} %select_n.11, f32[33,1024]{1,0:T(8,128)S(1)} %get-tuple-element.223, f32[512,1024]{1,0:T(8,128)S(1)} %fusion.38, f32[1024]{0:T(1024)S(1)} %get-tuple-element.220, f32[512]{0:T(512)S(1)} %dynamic_slice.29), kind=kOutput, calls=%fused_computation.8.clone.1 | convolution fusion | flops 209732096 | bytes 2430980 | tf_op jit(solution)/shard_map/while/body/eval_jaxpr/dot_general | solution.py:109
  47.8 1.8 %fusion.38 = f32[512,1024]{1,0:T(8,128)S(1)} fusion(f32[16,1024]{1,0:T(8,128)S(1)} %get-tuple-element.222, f32[16,4096]{1,0:T(8,128)S(1)} %get-tuple-element.221, s32[]{:T(128)S(6)} %select_n.11), kind=kOutput, calls=%fused_computation.13.clone.1 | convolution fusion | flops 100663296 | bytes 2195460 | tf_op jit(solution)/shard_map/while/body/eval_jaxpr/dot_general | solution.py:101
  49.7 2.5 %fusion.39 = f32[33,4096]{1,0:T(8,128)S(1)} fusion(f32[33,4096]{1,0:T(8,128)S(1)} %get-tuple-element.207, s32[]{:T(128)S(6)} %select_n.11, f32[33,1024]{1,0:T(8,128)S(1)} %get-tuple-element.223, f32[512,1024]{1,0:T(8,128)S(1)} %fusion.38, f32[1024]{0:T(1024)S(1)} %get-tuple-element.220, f32[512]{0:T(512)S(1)} %dynamic_slice.29), kind=kOutput, calls=%fused_computation.8.clone.1 | convolution fusion | flops 209732096 | bytes 2430980 | tf_op jit(solution)/shard_map/while/body/eval_jaxpr/dot_general | solution.py:109
  52.3 1.8 %fusion.38 = f32[512,1024]{1,0:T(8,128)S(1)} fusion(f32[16,1024]{1,0:T(8,128)S(1)} %get-tuple-element.222, f32[16,4096]{1,0:T(8,128)S(1)} %get-tuple-element.221, s32[]{:T(128)S(6)} %select_n.11), kind=kOutput, calls=%fused_computation.13.clone.1 | convolution fusion | flops 100663296 | bytes 2195460 | tf_op jit(solution)/shard_map/while/body/eval_jaxpr/dot_general | solution.py:101
  54.1 2.5 %fusion.39 = f32[33,4096]{1,0:T(8,128)S(1)} fusion(f32[33,4096]{1,0:T(8,128)S(1)} %get-tuple-element.207, s32[]{:T(128)S(6)} %select_n.11, f32[33,1024]{1,0:T(8,128)S(1)} %get-tuple-element.223, f32[512,1024]{1,0:T(8,128)S(1)} %fusion.38, f32[1024]{0:T(1024)S(1)} %get-tuple-element.220, f32[512]{0:T(512)S(1)} %dynamic_slice.29), kind=kOutput, calls=%fused_computation.8.clone.1 | convolution fusion | flops 209732096 | bytes 2430980 | tf_op jit(solution)/shard_map/while/body/eval_jaxpr/dot_general | solution.py:109
  56.8 1.8 %fusion.38 = f32[512,1024]{1,0:T(8,128)S(1)} fusion(f32[16,1024]{1,0:T(8,128)S(1)} %get-tuple-element.222, f32[16,4096]{1,0:T(8,128)S(1)} %get-tuple-element.221, s32[]{:T(128)S(6)} %select_n.11), kind=kOutput, calls=%fused_computation.13.clone.1 | convolution fusion | flops 100663296 | bytes 2195460 | tf_op jit(solution)/shard_map/while/body/eval_jaxpr/dot_general | solution.py:101
  58.6 2.5 %fusion.39 = f32[33,4096]{1,0:T(8,128)S(1)} fusion(f32[33,4096]{1,0:T(8,128)S(1)} %get-tuple-element.207, s32[]{:T(128)S(6)} %select_n.11, f32[33,1024]{1,0:T(8,128)S(1)} %get-tuple-element.223, f32[512,1024]{1,0:T(8,128)S(1)} %fusion.38, f32[1024]{0:T(1024)S(1)} %get-tuple-element.220, f32[512]{0:T(512)S(1)} %dynamic_slice.29), kind=kOutput, calls=%fused_computation.8.clone.1 | convolution fusion | flops 209732096 | bytes 2430980 | tf_op jit(solution)/shard_map/while/body/eval_jaxpr/dot_general | solution.py:109
  61.2 1.8 %fusion.38 = f32[512,1024]{1,0:T(8,128)S(1)} fusion(f32[16,1024]{1,0:T(8,128)S(1)} %get-tuple-element.222, f32[16,4096]{1,0:T(8,128)S(1)} %get-tuple-element.221, s32[]{:T(128)S(6)} %select_n.11), kind=kOutput, calls=%fused_computation.13.clone.1 | convolution fusion | flops 100663296 | bytes 2195460 | tf_op jit(solution)/shard_map/while/body/eval_jaxpr/dot_general | solution.py:101
  63.1 2.5 %fusion.39 = f32[33,4096]{1,0:T(8,128)S(1)} fusion(f32[33,4096]{1,0:T(8,128)S(1)} %get-tuple-element.207, s32[]{:T(128)S(6)} %select_n.11, f32[33,1024]{1,0:T(8,128)S(1)} %get-tuple-element.223, f32[512,1024]{1,0:T(8,128)S(1)} %fusion.38, f32[1024]{0:T(1024)S(1)} %get-tuple-element.220, f32[512]{0:T(512)S(1)} %dynamic_slice.29), kind=kOutput, calls=%fused_computation.8.clone.1 | convolution fusion | flops 209732096 | bytes 2430980 | tf_op jit(solution)/shard_map/while/body/eval_jaxpr/dot_general | solution.py:109
  66.9 9.8 %all-to-all-start.1 = ((f32[32,17,128]{2,1,0:T(8,128)}), f32[32,17,128]{2,1,0:T(8,128)S(1)}, u32[]{:S(2)}, u32[]{:S(2)}) async-start(f32[32,17,128]{2,1,0:T(8,128)} %copy.9), calls=%async_computation.1 | async-start | bytes 786432 | tf_op jit(solution)/shard_map/all_to_all | solution.py:43
  76.7 10.1 %psum.28 = f32[16]{0:T(128)S(1)} all-reduce(f32[16]{0:T(128)S(1)} %get-tuple-element.142), channel_id=1, replica_groups=mesh['row_0'=4,'row_1'=2,'col_0'=8,'col_1'=4] {'row_0'}, use_global_device_ids=true, to_apply=%region_6.0 | all-reduce | flops 16 | bytes 128 | tf_op jit(solution)/shard_map/psum | solution.py:49
  86.8 2.5 %psum.29 = f32[16]{0:T(128)S(1)} all-reduce(f32[16]{0:T(128)S(1)} %psum.28), channel_id=1, replica_groups=mesh['row_0'=4,'row_1'=2,'col_0'=8,'col_1'=4] {'row_1'}, use_global_device_ids=true, to_apply=%region_7.0 | all-reduce | flops 16 | bytes 128 | tf_op jit(solution)/shard_map/psum | solution.py:49
  89.3 15.6 %psum.30 = f32[16]{0:T(128)S(1)} all-reduce(f32[16]{0:T(128)S(1)} %psum.29), channel_id=1, replica_groups=mesh['row_0'=4,'row_1'=2,'col_0'=8,'col_1'=4] {'col_0'}, use_global_device_ids=true, to_apply=%region_8.0 | all-reduce | flops 16 | bytes 128 | tf_op jit(solution)/shard_map/psum | solution.py:49
  104.9 10.4 %psum.31 = f32[16]{0:T(128)S(1)} all-reduce(f32[16]{0:T(128)S(1)} %psum.30), channel_id=1, replica_groups=mesh['row_0'=4,'row_1'=2,'col_0'=8,'col_1'=4] {'col_1'}, use_global_device_ids=true, to_apply=%region_9.0 | all-reduce | flops 16 | bytes 128 | tf_op jit(solution)/shard_map/psum | solution.py:49
  (33 shorter events, 9.1 us)
Async XLA Ops:
  3.5 26.2 %all-to-all-start = ((f32[32,17,128]{2,1,0:T(8,128)}), f32[32,17,128]{2,1,0:T(8,128)S(1)}, u32[]{:S(2)}, u32[]{:S(2)}) async-start(f32[32,17,128]{2,1,0:T(8,128)} %broadcast_in_dim.21), calls=%async_computation | async-start | bytes 786432 | tf_op jit(solution)/shard_map/all_to_all | solution.py:15
  66.9 49.0 %all-to-all-start.1 = ((f32[32,17,128]{2,1,0:T(8,128)}), f32[32,17,128]{2,1,0:T(8,128)S(1)}, u32[]{:S(2)}, u32[]{:S(2)}) async-start(f32[32,17,128]{2,1,0:T(8,128)} %copy.9), calls=%async_computation.1 | async-start | bytes 786432 | tf_op jit(solution)/shard_map/all_to_all | solution.py:43
where the time goes:
time: 118 us; the launch traced here: 117 us
  blocking collectives  52.7 us (45%)
  matrix products  34.9 us (30%)
  starting transfers between devices  21.1 us (18%)
  other arithmetic  3.68 us (3%)
  local copies, waits for them, and re-layouts  3.57 us (3%)
    psum x4, blocking collectives, one_axis_at_a_time(): x = lax.psum(x, axis)  38.7 us
    dot_general x8, matrix products, add_block(): lax.dot_general(values, kernel, (((1,), (1,)), ((), ())), precision=lax.P...  20.2 us
    dot_general x8, matrix products, add_block(): lax.dot_general(row_block, col_scaled, (((0,), (0,)), ((), ())), precisio...  14.7 us
    all_gather x2, blocking collectives, gathered_by_axis(): result = lax.all_gather(result, axes[number], axis=dim, tiled=True)  14.1 us
    all_to_all x1, starting transfers between devices, copy_for_each(): return lax.all_to_all(copies, axis, split_axis=0, concat_axis=0, tiled=True)  11.4 us
    all_to_all x1, starting transfers between devices, sent_and_summed(): lax.all_to_all(blocks, axis, split_axis=0, concat_axis=0, tiled=True)  9.79 us
  transfers between devices with their start and end apart: 2, of which 0 were waited for; matrix products, arithmetic and copies ran while one was open for 1% of the time, Pallas kernels for 0%

commit v1 on v0

v1 whole, which is shorter than its diff:
```python
import functools
import math

import jax
import jax.numpy as jnp
from jax import lax
from jax.experimental import pallas as pl
from jax.experimental.pallas import tpu as pltpu
from jax.sharding import Mesh
from jax.sharding import PartitionSpec as P

ROW = ("row_0", "row_1")
COL = ("col_0", "col_1")
ROW_COL = ("row_0", "row_1", "col_0", "col_1")
COL_ROW = ("col_0", "col_1", "row_0", "row_1")
LOG2E = math.log2(math.e)
LANES = 128
TILE = 256


def split3(x):
    high = x.astype(jnp.bfloat16).astype(jnp.float32)
    rest = x - high
    middle = rest.astype(jnp.bfloat16).astype(jnp.float32)
    return high, middle, rest - middle


def placed_rows(entries, height, lanes):
    row = lax.broadcasted_iota(jnp.int32, (height, lanes), 0)
    block = jnp.zeros((height, lanes), jnp.float32)
    for k, entry in enumerate(entries):
        block = jnp.where(row == k, entry, block)
    return block


def inverse_scales(scale_ref, dims):
    scales = jnp.broadcast_to(scale_ref[:, :dims], (dims, dims))
    row = lax.broadcasted_iota(jnp.int32, (dims, dims), 0)
    lane = lax.broadcasted_iota(jnp.int32, (dims, dims), 1)
    column = jnp.sum(jnp.where(row == lane, scales, 0.0), 1, keepdims=True)
    return 1.0 / column


def tile_kernel(rows_ref, cols_ref, scale_ref, out_ref, a_ref, b_ref, v_ref):
    row_chunks, entries, lanes = rows_ref.shape
    col_chunks = cols_ref.shape[0]
    dims = entries - 1
    bf16 = jnp.bfloat16
    inverse = inverse_scales(scale_ref, dims)
    root = math.sqrt(LOG2E)

    for p in range(row_chunks):
        scaled = rows_ref[p, :dims, :] * inverse * root
        norm = -0.5 * jnp.sum(scaled * scaled, 0, keepdims=True)
        h, m, l = split3(scaled)
        nh, nm, nl = split3(norm)
        norms = placed_rows((nh, nm, nl, 1.0, 1.0, 1.0), dims, lanes)
        blocks = (h, h, m, m, h, l, norms, jnp.zeros_like(norms))
        for g, block in enumerate(blocks):
            a_ref[g * dims:(g + 1) * dims, p * lanes:(p + 1) * lanes] = block.astype(bf16)

    def prepare(p, carry):
        unit = cols_ref[p, :dims, :] * inverse
        alpha = cols_ref[p, dims:dims + 1, :]
        scaled = unit * root
        norm = -0.5 * jnp.sum(scaled * scaled, 0, keepdims=True)
        h, m, l = split3(scaled)
        nh, nm, nl = split3(norm)
        norms = placed_rows((1.0, 1.0, 1.0, nh, nm, nl), dims, lanes)
        stacked = jnp.concatenate([h, m, h, m, l, h, norms, jnp.zeros_like(norms)], 0)
        start = pl.multiple_of(p * lanes, lanes)
        b_ref[pl.ds(start, lanes), :] = stacked.T.astype(bf16)
        fh, fm, fl = split3(alpha * unit)
        sh, sm, sl = split3(alpha * unit * unit)
        alphas = placed_rows(split3(alpha), dims, lanes)
        for g, block in enumerate((fh, fm, sh, sm, alphas, fl, sl)):
            v_ref[g * dims:(g + 1) * dims, pl.ds(start, lanes)] = block.astype(bf16)
        return carry

    lax.fori_loop(0, col_chunks, prepare, 0, unroll=4)

    col_count = col_chunks * lanes
    grad = jnp.zeros((dims, lanes), jnp.float32)
    for t in range(row_chunks * lanes // TILE):
        a_tile = a_ref[:, t * TILE:(t + 1) * TILE]

        def step(c, total):
            start = pl.multiple_of(c * STEP, STEP)
            exponent = jnp.dot(b_ref[pl.ds(start, STEP), :], a_tile, preferred_element_type=jnp.float32)
            kernel = jnp.exp2(exponent)
            high = kernel.astype(bf16)
            low = (kernel - high.astype(jnp.float32)).astype(bf16)
            from_high = jnp.dot(v_ref[:, pl.ds(start, STEP)], high, preferred_element_type=jnp.float32)
            from_low = jnp.dot(v_ref[:5 * dims, pl.ds(start, STEP)], low, preferred_element_type=jnp.float32)
            return total[0] + from_high, total[1] + from_low

        zeros = (jnp.zeros((7 * dims, TILE), jnp.float32), jnp.zeros((5 * dims, TILE), jnp.float32))
        big, small = lax.fori_loop(0, col_count // STEP, step, zeros, unroll=UNROLL)
        part = lambda x, g: x[g * dims:(g + 1) * dims]
        first = (part(small, 0) + part(small, 1) + part(big, 5)) + part(big, 1) + part(big, 0)
        second = (part(small, 2) + part(small, 3) + part(big, 6)) + part(big, 3) + part(big, 2)
        weights = part(big, 4) + part(small, 4)
        weight = weights[0:1] + weights[1:2] + weights[2:3]
        for q in range(TILE // lanes):
            p = t * (TILE // lanes) + q
            cut = slice(q * lanes, (q + 1) * lanes)
            scaled = rows_ref[p, :dims, :] * inverse
            row_alpha = rows_ref[p, dims:dims + 1, :]
            terms = 0.5 * row_alpha * (scaled * scaled * weight[:, cut] - 2.0 * scaled * first[:, cut] + second[:, cut])
            out_ref[p, :dims, :] = terms
            out_ref[p, dims:dims + 1, :] = weight[:, cut]
            grad = grad + terms
    column = jnp.sum(grad, 1, keepdims=True)
    row = lax.broadcasted_iota(jnp.int32, (dims, lanes), 0)
    lane = lax.broadcasted_iota(jnp.int32, (dims, lanes), 1)
    shares = jnp.sum(jnp.where(row == lane, column, 0.0), 0, keepdims=True)
    for p in range(row_chunks):
        out_ref[p, dims + 1:dims + 2, :] = shares


STEP = 512
UNROLL = 2


def tile_terms(rows, cols, lengthscale):
    row_chunks, entries, lanes = rows.shape
    col_chunks = cols.shape[0]
    dims = entries - 1
    whole = pl.BlockSpec(memory_space=pltpu.VMEM)
    pairs = row_chunks * col_chunks * lanes * lanes
    return pl.pallas_call(
        tile_kernel,
        out_shape=jax.ShapeDtypeStruct((row_chunks, entries + 1, lanes), jnp.float32),
        in_specs=[whole, whole, whole],
        out_specs=whole,
        scratch_shapes=[
            pltpu.VMEM((8 * dims, row_chunks * lanes), jnp.bfloat16),
            pltpu.VMEM((col_chunks * lanes, 8 * dims), jnp.bfloat16),
            pltpu.VMEM((7 * dims, col_chunks * lanes), jnp.bfloat16),
        ],
        cost_estimate=pl.CostEstimate(flops=600 * pairs, bytes_accessed=1 << 20, transcendentals=pairs),
        name="tile_terms",
    )(rows, cols, lengthscale.reshape(1, dims))


def copies(x, axes):
    blocks = jnp.broadcast_to(x, (lax.axis_size(axes), *x.shape))
    return lax.all_to_all(blocks, axes, split_axis=0, concat_axis=0, tiled=True)


def on_device(x_rows, alpha_rows, x_cols, alpha_cols, lengthscale):
    dims = x_rows.shape[0]
    rows = copies(jnp.concatenate([x_rows, alpha_rows[None, :]], 0), ROW)
    cols = copies(jnp.concatenate([x_cols, alpha_cols[None, :]], 0), COL)
    parts = tile_terms(rows, cols, lengthscale)
    arrived = lax.all_to_all(parts, ROW, split_axis=0, concat_axis=0, tiled=True)
    summed = arrived.sum(axis=0)
    shares = copies(summed[dims + 1:], COL)
    total_rows = x_rows.shape[1] * lax.axis_size(ROW_COL)
    grad = shares.sum(axis=(0, 1))[:dims] / total_rows
    return summed[:dims], summed[dims], grad


def solution(mesh):
    finer = Mesh(mesh.devices.reshape(4, 2, 8, 4), ROW_COL)
    in_specs = (P(None, ROW_COL), P(ROW_COL), P(None, COL_ROW), P(COL_ROW), P())
    out_specs = (P(None, ROW_COL), P(ROW_COL), P())
    return jax.shard_map(on_device, mesh=finer, in_specs=in_specs, out_specs=out_specs, check_vma=False)
```

time: 118 us -> 77.5 us (0.66)
  the two profiles are of different devices: /device:TPU:32 before, /device:TPU:1 now
where the time goes in v1:
time: 77.5 us; the launch traced here: 77 us
  blocking collectives  35 us (45%)
  Pallas kernels  12.9 us (17%)
  waiting for transfers between devices  12.4 us (16%)
  starting transfers between devices  10.5 us (14%)
  local copies, waits for them, and re-layouts  4.29 us (6%)
  other arithmetic  1.25 us (2%)
    all_to_all x1, blocking collectives, copies(): return lax.all_to_all(blocks, axes, split_axis=0, concat_axis=0, tiled=True)  24.3 us
    pallas_call x1, Pallas kernels, tile_terms(): pl.pallas_call(tile_kernel, out_shape=jax.ShapeDtypeStruct((row_chunks, e...  12.9 us
    all_to_all x2, waiting for transfers between devices, copies(): return lax.all_to_all(blocks, axes, split_axis=0, concat_axis=0, tiled=True)  12.4 us
    all_to_all x1, blocking collectives, on_device(): lax.all_to_all(parts, ROW, split_axis=0, concat_axis=0, tiled=True)  10.7 us
    all_to_all x2, starting transfers between devices, copies(): return lax.all_to_all(blocks, axes, split_axis=0, concat_axis=0, tiled=True)  10.5 us
    unnamed x8, local copies, waits for them, and re-layouts  1.9 us
  transfers between devices with their start and end apart: 2, of which 2 were waited for; matrix products, arithmetic and copies ran while one was open for 1% of the time, Pallas kernels for 0%

profile of v1, /device:TPU:1, one launch (start us, length us, event | category | flops | bytes accessed | tf_op | source)
XLA Modules:
  0.0 77.0 jit_solution(12055175381224954203)
XLA Ops:
  0.6 0.0 copy-start.2
  0.6 0.6 copy-done.2
  1.3 0.7 pad_maximum_fusion
  2.0 0.6 broadcast_in_dim.16
  2.6 0.0 copy-start.1
  2.6 6.6 %all-to-all-start = ((f32[8,17,128]{2,1,0:T(8,128)}), f32[8,17,128]{2,1,0:T(8,128)S(1)}, u32[]{:S(2)}, u32[]{:S(2)}) async-start(f32[8,17,128]{2,1,0:T(8,128)} %broadcast_in_dim.16), calls=%async_computation | async-start | bytes 196608 | tf_op jit(solution)/shard_map/all_to_all | solution.py:148
  9.2 0.0 copy-start.3
  9.2 0.0 copy-done.1
  9.2 0.7 copy-done.3
  9.9 4.3 %all-to-all-done.rows_ref = f32[8,17,128]{2,1,0:T(8,128)S(1)} async-done(((f32[8,17,128]{2,1,0:T(8,128)}), f32[8,17,128]{2,1,0:T(8,128)S(1)}, u32[]{:S(2)}, u32[]{:S(2)}) %all-to-all-start) | async-done | bytes 69664 | tf_op jit(solution)/shard_map/all_to_all | solution.py:148
  14.2 0.0 copy-start
  14.3 0.6 copy-done
  14.9 24.3 %all_to_all.20.cols_ref = f32[32,17,128]{2,1,0:T(8,128)} all-to-all(f32[32,17,128]{2,1,0:T(8,128)S(1)} %broadcast_in_dim.18), channel_id=1, replica_groups=mesh['row_0'=4,'row_1'=2,'col_0'=8,'col_1'=4] {'col_0','col_1'}, dimensions={0} | all-to-all | bytes 557056 | tf_op jit(solution)/shard_map/all_to_all | solution.py:148
  39.2 12.9 %tile_terms.1 = f32[8,18,128]{2,1,0:T(8,128)} custom-call(f32[8,17,128]{2,1,0:T(8,128)} %copy-done, f32[32,17,128]{2,1,0:T(8,128)} %all_to_all.20.cols_ref, f32[1,16]{1,0:T(1,128)} %bitcast.11), custom_call_target="tpu_custom_call" | custom-call | flops 2516582400 | bytes 1048576 | tf_op jit(solution)/shard_map/tile_terms/pallas_call | solution.py:131
  52.1 10.7 %all_to_all.21 = f32[8,18,128]{2,1,0:T(8,128)S(1)} all-to-all(f32[8,18,128]{2,1,0:T(8,128)} %tile_terms.1), channel_id=1, replica_groups=mesh['row_0'=4,'row_1'=2,'col_0'=8,'col_1'=4] {'row_0','row_1'}, dimensions={0} | all-to-all | bytes 147456 | tf_op jit(solution)/shard_map/all_to_all | solution.py:156
  62.8 0.5 slice_bitcast_fusion
  63.3 0.6 broadcast_in_dim.19
  63.9 3.9 %all-to-all-start.3 = ((f32[32,1,128]{2,1,0:T(1,128)}), f32[32,1,128]{2,1,0:T(1,128)S(1)}, u32[]{:S(2)}, u32[]{:S(2)}) async-start(f32[32,1,128]{2,1,0:T(1,128)} %broadcast_in_dim.19), calls=%async_computation.3 | async-start | bytes 32768 | tf_op jit(solution)/shard_map/all_to_all | solution.py:148
  67.8 0.6 slice.19
  68.4 8.0 %all-to-all-done.3 = f32[32,1,128]{2,1,0:T(1,128)S(1)} async-done(((f32[32,1,128]{2,1,0:T(1,128)}), f32[32,1,128]{2,1,0:T(1,128)S(1)}, u32[]{:S(2)}, u32[]{:S(2)}) %all-to-all-start.3) | async-done | bytes 16416 | tf_op jit(solution)/shard_map/all_to_all | solution.py:148
  76.5 0.5 slice_multiply_fusion
  (4 shorter events, 0.1 us)
Async XLA Ops:
  0.6 0.7 copy-start.2
  2.6 6.6 %copy-start.1 = (f32[16,128]{1,0:T(8,128)S(1)}, f32[16,128]{1,0:T(8,128)}, u32[]{:S(2)}) copy-start(f32[16,128]{1,0:T(8,128)} %param.7) | copy-start | bytes 24580
  2.6 11.6 %all-to-all-start = ((f32[8,17,128]{2,1,0:T(8,128)}), f32[8,17,128]{2,1,0:T(8,128)S(1)}, u32[]{:S(2)}, u32[]{:S(2)}) async-start(f32[8,17,128]{2,1,0:T(8,128)} %broadcast_in_dim.16), calls=%async_computation | async-start | bytes 196608 | tf_op jit(solution)/shard_map/all_to_all | solution.py:148
  9.2 0.7 copy-start.3
  14.2 0.6 copy-start
  63.9 12.6 %all-to-all-start.3 = ((f32[32,1,128]{2,1,0:T(1,128)}), f32[32,1,128]{2,1,0:T(1,128)S(1)}, u32[]{:S(2)}, u32[]{:S(2)}) async-start(f32[32,1,128]{2,1,0:T(1,128)} %broadcast_in_dim.19), calls=%async_computation.3 | async-start | bytes 32768 | tf_op jit(solution)/shard_map/all_to_all | solution.py:148

commit v2 on v1

v2 whole, which is shorter than its diff:
```python
import math

import jax
import jax.numpy as jnp
from jax import lax
from jax.experimental import pallas as pl
from jax.experimental.pallas import tpu as pltpu
from jax.sharding import Mesh
from jax.sharding import PartitionSpec as P

ROW_COL = ("row_0", "row_1", "col_0", "col_1")
COL_ROW = ("col_0", "col_1", "row_0", "row_1")
LOG2E = math.log2(math.e)
LANES = 128
COL_CLASSES = 8
STEP = 512
UNROLL = 2


def split3(x):
    high = x.astype(jnp.bfloat16).astype(jnp.float32)
    rest = x - high
    middle = rest.astype(jnp.bfloat16).astype(jnp.float32)
    return high, middle, rest - middle


def placed_rows(entries, height, lanes):
    row = lax.broadcasted_iota(jnp.int32, (height, lanes), 0)
    block = jnp.zeros((height, lanes), jnp.float32)
    for k, entry in enumerate(entries):
        block = jnp.where(row == k, entry, block)
    return block


def to_left(x, lanes):
    return pltpu.roll(x, (LANES - lanes) % LANES, 1)


def to_right(x, lanes):
    return pltpu.roll(x, lanes % LANES, 1)


class Plan:
    def __init__(self, devices, dims, points):
        self.devices, self.dims = devices, dims
        self.cols = COL_CLASSES
        self.rows = devices // self.cols
        self.row_each = points // self.rows
        self.col_each = points // self.cols
        self.at_cols = self.row_each * dims
        self.at_col_alpha = self.at_cols + self.col_each * dims
        self.at_row_alpha = self.at_col_alpha + self.col_each
        self.tiles = pl.cdiv(self.at_row_alpha + self.row_each, LANES)
        self.at_weight = self.row_each * dims
        self.at_grad = self.at_weight + pl.cdiv(self.row_each, 8) * 8


def spread_kernel(plan, rows_ref, row_alpha_ref, cols_ref, col_alpha_ref, scale_ref, out_ref):
    dims = plan.dims
    scales = jnp.broadcast_to(scale_ref[:, :dims], (dims, dims))
    down = lax.broadcasted_iota(jnp.int32, (dims, dims), 0)
    along = lax.broadcasted_iota(jnp.int32, (dims, dims), 1)
    inverse = 1.0 / jnp.sum(jnp.where(down == along, scales, 0.0), 1, keepdims=True)
    rows = rows_ref[...] * inverse
    cols = cols_ref[...] * inverse
    pieces = [to_left(rows, i * plan.rows) for i in range(plan.row_each)]
    pieces += [to_left(cols, i * plan.cols) for i in range(plan.col_each)]
    alphas = [to_left(col_alpha_ref[...], i * plan.cols) for i in range(plan.col_each)]
    alphas += [to_left(row_alpha_ref[...], i * plan.rows) for i in range(plan.row_each)]
    left = plan.tiles * LANES - plan.at_col_alpha
    pieces.append(placed_rows(alphas, left, LANES))
    stacked = jnp.concatenate(pieces, 0)
    for k in range(plan.tiles):
        turned = stacked[k * LANES:(k + 1) * LANES].T
        lane = lax.broadcasted_iota(jnp.int32, (plan.cols, LANES), 1) + k * LANES
        is_row = (lane < plan.at_cols) | (lane >= plan.at_row_alpha)
        of_cols = turned[:plan.cols]
        for r in range(plan.rows):
            of_row = jnp.broadcast_to(turned[r:r + 1], (plan.cols, LANES))
            start = r * plan.cols * plan.tiles + k
            out_ref[pl.ds(start, plan.cols, stride=plan.tiles), :] = jnp.where(is_row, of_row, of_cols)


def tile_kernel(plan, in_ref, out_ref, t_ref, a_ref, b_ref, v_ref, o_ref):
    dims, width = plan.dims, plan.devices
    bf16 = jnp.bfloat16
    root = math.sqrt(LOG2E)
    for k in range(plan.tiles):
        t_ref[k * LANES:(k + 1) * LANES, :] = in_ref[pl.ds(k, width, stride=plan.tiles), :].T

    def exponents(unit, ones_first):
        scaled = unit * root
        norm = -0.5 * jnp.sum(scaled * scaled, 0, keepdims=True)
        parts = split3(norm)
        ones = (1.0, 1.0, 1.0)
        norms = placed_rows(ones + parts if ones_first else parts + ones, dims, width)
        return *split3(scaled), norms

    for i in range(plan.row_each):
        h, m, l, norms = exponents(t_ref[i * dims:(i + 1) * dims, :], False)
        blocks = (h, h, m, m, h, l, norms, jnp.zeros_like(norms))
        for g, block in enumerate(blocks):
            a_ref[g * dims:(g + 1) * dims, i * width:(i + 1) * width] = block.astype(bf16)

    for i in range(plan.col_each):
        at = plan.at_cols + i * dims
        unit = t_ref[at:at + dims, :]
        alpha = t_ref[plan.at_col_alpha + i:plan.at_col_alpha + i + 1, :]
        h, m, l, norms = exponents(unit, True)
        stacked = jnp.concatenate([h, m, h, m, l, h, norms, jnp.zeros_like(norms)], 0)
        b_ref[i * width:(i + 1) * width, :] = stacked.astype(bf16).T
        weighted = alpha * unit
        fh, fm, fl = split3(weighted)
        sh, sm, sl = split3(weighted * unit)
        alphas = placed_rows(split3(alpha), dims, width)
        for g, block in enumerate((fh, fm, sh, sm, alphas, fl, sl)):
            v_ref[g * dims:(g + 1) * dims, i * width:(i + 1) * width] = block.astype(bf16)

    col_count = plan.col_each * width
    grad = jnp.zeros((dims, width), jnp.float32)
    o_ref[plan.at_weight:, :] = jnp.zeros((LANES - plan.at_weight, width), jnp.float32)
    for i in range(plan.row_each):
        a_tile = a_ref[:, i * width:(i + 1) * width]

        def step(c, total):
            start = pl.multiple_of(c * STEP, STEP)
            exponent = jnp.dot(b_ref[pl.ds(start, STEP), :], a_tile, preferred_element_type=jnp.float32)
            kernel = jnp.exp2(exponent)
            high = kernel.astype(bf16)
            low = (kernel - high.astype(jnp.float32)).astype(bf16)
            from_high = jnp.dot(v_ref[:, pl.ds(start, STEP)], high, preferred_element_type=jnp.float32)
            from_low = jnp.dot(v_ref[:5 * dims, pl.ds(start, STEP)], low, preferred_element_type=jnp.float32)
            return total[0] + from_high, total[1] + from_low

        zeros = (jnp.zeros((7 * dims, width), jnp.float32), jnp.zeros((5 * dims, width), jnp.float32))
        big, small = lax.fori_loop(0, col_count // STEP, step, zeros, unroll=UNROLL)

        def part(x, g):
            return x[g * dims:(g + 1) * dims]

        first = (part(small, 0) + part(small, 1) + part(big, 5)) + part(big, 1) + part(big, 0)
        second = (part(small, 2) + part(small, 3) + part(big, 6)) + part(big, 3) + part(big, 2)
        weights = part(big, 4) + part(small, 4)
        weight = weights[0:1] + weights[1:2] + weights[2:3]
        unit = t_ref[i * dims:(i + 1) * dims, :]
        alpha = t_ref[plan.at_row_alpha + i:plan.at_row_alpha + i + 1, :]
        terms = 0.5 * alpha * (unit * unit * weight - 2.0 * unit * first + second)
        o_ref[i * dims:(i + 1) * dims, :] = terms
        o_ref[plan.at_weight + i:plan.at_weight + i + 1, :] = weight
        grad = grad + terms
    share = jnp.sum(grad, 1, keepdims=True)
    o_ref[plan.at_grad:plan.at_grad + dims, :] = jnp.broadcast_to(share, (dims, width))
    out_ref[...] = o_ref[...].T


def finish_kernel(plan, total_rows, in_ref, terms_ref, weight_ref, grad_ref):
    dims = plan.dims
    summed = jnp.sum(in_ref[...].reshape(plan.rows, plan.cols, LANES), 1)
    total = jnp.sum(summed, 0, keepdims=True)
    padded = jnp.concatenate([summed, jnp.zeros((LANES - plan.rows, LANES), jnp.float32)], 0)
    turned = padded.T
    terms = turned[:dims]
    weight = turned[plan.at_weight:plan.at_weight + 1]
    for i in range(1, plan.row_each):
        terms = terms + to_right(turned[i * dims:(i + 1) * dims], i * plan.rows)
        weight = weight + to_right(turned[plan.at_weight + i:plan.at_weight + i + 1], i * plan.rows)
    terms_ref[...] = terms
    weight_ref[...] = weight
    grad_ref[...] = to_left(total, plan.at_grad)[:, :dims] / total_rows


def on_device(x_rows, alpha_rows, x_cols, alpha_cols, lengthscale):
    dims, points = x_rows.shape
    devices = lax.axis_size(ROW_COL)
    plan = Plan(devices, dims, points)
    whole = pl.BlockSpec(memory_space=pltpu.VMEM)
    f32, bf16 = jnp.float32, jnp.bfloat16

    def exchanged(x, tiles):
        blocks = x.reshape(devices, 1, tiles * LANES)
        arrived = lax.all_to_all(blocks, ROW_COL, split_axis=0, concat_axis=0, tiled=True)
        return arrived.reshape(devices * tiles, LANES)

    blocks = pl.pallas_call(
        lambda *refs: spread_kernel(plan, *refs),
        out_shape=jax.ShapeDtypeStruct((devices * plan.tiles, LANES), f32),
        in_specs=[whole] * 5,
        out_specs=whole,
        name="spread",
    )(x_rows, alpha_rows.reshape(1, points), x_cols, alpha_cols.reshape(1, points), lengthscale.reshape(1, dims))
    gathered = exchanged(blocks, plan.tiles)
    row_count, col_count = plan.row_each * devices, plan.col_each * devices
    shares = pl.pallas_call(
        lambda *refs: tile_kernel(plan, *refs),
        out_shape=jax.ShapeDtypeStruct((devices, LANES), f32),
        in_specs=[whole],
        out_specs=whole,
        scratch_shapes=[
            pltpu.VMEM((plan.tiles * LANES, devices), f32),
            pltpu.VMEM((8 * dims, row_count), bf16),
            pltpu.VMEM((col_count, 8 * dims), bf16),
            pltpu.VMEM((7 * dims, col_count), bf16),
            pltpu.VMEM((LANES, devices), f32),
        ],
        name="tile",
    )(gathered)
    arrived = exchanged(shares, 1)
    terms, weight, grad = pl.pallas_call(
        lambda *refs: finish_kernel(plan, points * devices, *refs),
        out_shape=(
            jax.ShapeDtypeStruct((dims, points), f32),
            jax.ShapeDtypeStruct((1, points), f32),
            jax.ShapeDtypeStruct((1, dims), f32),
        ),
        in_specs=[whole],
        out_specs=(whole, whole, whole),
        name="finish",
    )(arrived)
    return terms, weight.reshape(points), grad.reshape(dims)


def solution(mesh):
    finer = Mesh(mesh.devices.reshape(4, 2, 8, 4), ROW_COL)
    in_specs = (P(None, ROW_COL), P(ROW_COL), P(None, COL_ROW), P(COL_ROW), P())
    out_specs = (P(None, ROW_COL), P(ROW_COL), P())
    return jax.shard_map(on_device, mesh=finer, in_specs=in_specs, out_specs=out_specs, check_vma=False)
```

time: 77.5 us -> 70.1 us (0.905)
  blocking collectives: 35 us -> 53.3 us
  waiting for transfers between devices: 12.4 us -> 0 us
  starting transfers between devices: 10.5 us -> 0 us
  local copies, waits for them, and re-layouts: 4.29 us -> 0 us
  Pallas kernels: 12.9 us -> 15.9 us
  other arithmetic: 1.25 us -> 0 us
    all_to_all x2, blocking collectives: 35 us -> 53.3 us  [exchanged(): lax.all_to_all(blocks, ROW_COL, split_axis=0, concat_axis=0, tiled=True)]
    all_to_all x2 -> x0, waiting for transfers between devices: 12.4 us -> none  [copies(): return lax.all_to_all(blocks, axes, split_axis=0, concat_axis=0, tiled=True)]
    all_to_all x2 -> x0, starting transfers between devices: 10.5 us -> none  [copies(): return lax.all_to_all(blocks, axes, split_axis=0, concat_axis=0, tiled=True)]
    pallas_call x1 -> x3, Pallas kernels: 12.9 us -> 15.9 us  [the longest x1 12.4 us: on_device(): pl.pallas_call(lambda *refs: tile_kernel(plan, *refs), out_shape=jax.Shap...]
    unnamed x8 -> x0, local copies, waits for them, and re-layouts: 1.9 us -> none
    broadcast_in_dim x3 -> x0, local copies, waits for them, and re-layouts: 1.27 us -> none  [copies(): blocks = jnp.broadcast_to(x, (lax.axis_size(axes), *x.shape))]
    slice x2 -> x0, local copies, waits for them, and re-layouts: 1.11 us -> none  [the longest x1 0.6 us: on_device(): return (summed[:dims], summed[dims], grad)]
  transfers between devices with their start and end apart: 2 -> 0, of which waited for: 2 -> 0; matrix products, arithmetic and copies ran while one was open for 1% -> 0% of each run, Pallas kernels for 0% -> 0%
where the time goes in v2:
time: 70.1 us; the launch traced here: 69.8 us
  blocking collectives  53.3 us (76%)
  Pallas kernels  15.9 us (23%)
    all_to_all x2, blocking collectives, exchanged(): lax.all_to_all(blocks, ROW_COL, split_axis=0, concat_axis=0, tiled=True)  53.3 us
    pallas_call x1, Pallas kernels, on_device(): pl.pallas_call(lambda *refs: tile_kernel(plan, *refs), out_shape=jax.Shap...  12.4 us
    pallas_call x1, Pallas kernels, on_device(): pl.pallas_call(lambda *refs: spread_kernel(plan, *refs), out_shape=jax.Sh...  1.8 us
    pallas_call x1, Pallas kernels, on_device(): pl.pallas_call(lambda *refs: finish_kernel(plan, points * devices, *refs)...  1.68 us

profile of v2, /device:TPU:1, one launch (start us, length us, event | category | flops | bytes accessed | tf_op | source)
XLA Modules:
  0.0 69.8 jit_solution(12645930498141619248)
XLA Ops:
  0.6 1.8 %spread.1 = f32[768,128]{1,0:T(8,128)} custom-call(f32[16,128]{1,0:T(8,128)} %refs_0_.1, f32[1,128]{1,0:T(1,128)} %bitcast.15, f32[16,128]{1,0:T(8,128)} %refs_2_.1, f32[1,128]{1,0:T(1,128)} %bitcast.16, f32[1,16]{1,0:T(1,128)} %bitcast.17), custom_call_target="tpu_custom_call" | custom-call | tf_op jit(solution)/shard_map/spread/pallas_call | solution.py:184
  2.4 33.2 %all_to_all.10 = f32[256,1,384]{2,1,0:T(1,128)} all-to-all(f32[256,1,384]{2,1,0:T(1,128)} %bitcast.12), channel_id=1, replica_groups=mesh['row_0'=4,'row_1'=2,'col_0'=8,'col_1'=4] {'row_0','row_1','col_0','..., dimensions={0} | all-to-all | bytes 786432 | tf_op jit(solution)/shard_map/all_to_all | solution.py:181
  35.6 12.4 %tile.1 = f32[256,128]{1,0:T(8,128)} custom-call(f32[768,128]{1,0:T(8,128)} %bitcast.11), custom_call_target="tpu_custom_call" | custom-call | tf_op jit(solution)/shard_map/tile/pallas_call | solution.py:193
  48.0 20.1 %all_to_all.11 = f32[256,1,128]{2,1,0:T(1,128)} all-to-all(f32[256,1,128]{2,1,0:T(1,128)} %bitcast.14), channel_id=1, replica_groups=mesh['row_0'=4,'row_1'=2,'col_0'=8,'col_1'=4] {'row_0','row_1','col_0','..., dimensions={0} | all-to-all | bytes 262144 | tf_op jit(solution)/shard_map/all_to_all | solution.py:181
  68.1 1.7 %finish.1 = (f32[16,128]{1,0:T(8,128)}, f32[1,128]{1,0:T(1,128)}, f32[1,16]{1,0:T(1,128)}) custom-call(f32[256,128]{1,0:T(8,128)} %bitcast.13), custom_call_target="tpu_custom_call" | custom-call | tf_op jit(solution)/shard_map/finish/pallas_call | solution.py:208

commit v3 on v2

--- a/solution.py
+++ b/solution.py
@@ -14,7 +14,7 @@
 LANES = 128
 COL_CLASSES = 8
 STEP = 512
-UNROLL = 2
+UNROLL = 8
 
 
 def split3(x):

time: 70.1 us -> 64.7 us (0.923)
  Pallas kernels: 15.9 us -> 10.5 us
    pallas_call x1, Pallas kernels: 12.4 us -> 7.04 us  [on_device(): pl.pallas_call(lambda *refs: tile_kernel(plan, *refs), out_shape=jax.Shap...]
where the time goes in v3:
time: 64.7 us; the launch traced here: 64.5 us
  blocking collectives  53.3 us (82%)
  Pallas kernels  10.5 us (16%)
    all_to_all x2, blocking collectives, exchanged(): lax.all_to_all(blocks, ROW_COL, split_axis=0, concat_axis=0, tiled=True)  53.3 us
    pallas_call x1, Pallas kernels, on_device(): pl.pallas_call(lambda *refs: tile_kernel(plan, *refs), out_shape=jax.Shap...  7.04 us
    pallas_call x1, Pallas kernels, on_device(): pl.pallas_call(lambda *refs: spread_kernel(plan, *refs), out_shape=jax.Sh...  1.8 us
    pallas_call x1, Pallas kernels, on_device(): pl.pallas_call(lambda *refs: finish_kernel(plan, points * devices, *refs)...  1.68 us

profile of v3, /device:TPU:1, one launch (start us, length us, event | category | flops | bytes accessed | tf_op | source)
XLA Modules:
  0.0 64.5 jit_solution(15762992987150118085)
XLA Ops:
  0.6 1.8 %spread.1 = f32[768,128]{1,0:T(8,128)} custom-call(f32[16,128]{1,0:T(8,128)} %refs_0_.1, f32[1,128]{1,0:T(1,128)} %bitcast.15, f32[16,128]{1,0:T(8,128)} %refs_2_.1, f32[1,128]{1,0:T(1,128)} %bitcast.16, f32[1,16]{1,0:T(1,128)} %bitcast.17), custom_call_target="tpu_custom_call" | custom-call | tf_op jit(solution)/shard_map/spread/pallas_call | solution.py:184
  2.4 33.2 %all_to_all.10 = f32[256,1,384]{2,1,0:T(1,128)} all-to-all(f32[256,1,384]{2,1,0:T(1,128)} %bitcast.12), channel_id=1, replica_groups=mesh['row_0'=4,'row_1'=2,'col_0'=8,'col_1'=4] {'row_0','row_1','col_0','..., dimensions={0} | all-to-all | bytes 786432 | tf_op jit(solution)/shard_map/all_to_all | solution.py:181
  35.6 7.0 %tile.1 = f32[256,128]{1,0:T(8,128)} custom-call(f32[768,128]{1,0:T(8,128)} %bitcast.11), custom_call_target="tpu_custom_call" | custom-call | tf_op jit(solution)/shard_map/tile/pallas_call | solution.py:193
  42.7 20.1 %all_to_all.11 = f32[256,1,128]{2,1,0:T(1,128)} all-to-all(f32[256,1,128]{2,1,0:T(1,128)} %bitcast.14), channel_id=1, replica_groups=mesh['row_0'=4,'row_1'=2,'col_0'=8,'col_1'=4] {'row_0','row_1','col_0','..., dimensions={0} | all-to-all | bytes 262144 | tf_op jit(solution)/shard_map/all_to_all | solution.py:181
  62.8 1.7 %finish.1 = (f32[16,128]{1,0:T(8,128)}, f32[1,128]{1,0:T(1,128)}, f32[1,16]{1,0:T(1,128)}) custom-call(f32[256,128]{1,0:T(8,128)} %bitcast.13), custom_call_target="tpu_custom_call" | custom-call | tf_op jit(solution)/shard_map/finish/pallas_call | solution.py:208

commit v4 on v3

--- a/solution.py
+++ b/solution.py
@@ -186,6 +186,7 @@
         out_shape=jax.ShapeDtypeStruct((devices * plan.tiles, LANES), f32),
         in_specs=[whole] * 5,
         out_specs=whole,
+        compiler_params=pltpu.CompilerParams(vmem_limit_bytes=4 << 20),
         name="spread",
     )(x_rows, alpha_rows.reshape(1, points), x_cols, alpha_cols.reshape(1, points), lengthscale.reshape(1, dims))
     gathered = exchanged(blocks, plan.tiles)
@@ -202,6 +203,7 @@
             pltpu.VMEM((7 * dims, col_count), bf16),
             pltpu.VMEM((LANES, devices), f32),
         ],
+        compiler_params=pltpu.CompilerParams(vmem_limit_bytes=16 << 20),
         name="tile",
     )(gathered)
     arrived = exchanged(shares, 1)
@@ -214,6 +216,7 @@
         ),
         in_specs=[whole],
         out_specs=(whole, whole, whole),
+        compiler_params=pltpu.CompilerParams(vmem_limit_bytes=4 << 20),
         name="finish",
     )(arrived)
     return terms, weight.reshape(points), grad.reshape(dims)

time: 64.7 us -> 61 us (0.943)
  Pallas kernels: 10.5 us -> 6.46 us
  local copies, waits for them, and re-layouts: 0 us -> 2.06 us
  blocking collectives: 53.3 us -> 51.5 us
    unnamed x0 -> x10, local copies, waits for them, and re-layouts: none -> 2.06 us
    all_to_all x2, blocking collectives: 53.3 us -> 51.5 us  [exchanged(): lax.all_to_all(blocks, ROW_COL, split_axis=0, concat_axis=0, tiled=True)]
    pallas_call x1, Pallas kernels: 7.04 us -> 5.39 us  [on_device(): pl.pallas_call(lambda *refs: tile_kernel(plan, *refs), out_shape=jax.Shap...]
    pallas_call x1, Pallas kernels: 1.8 us -> 0.29 us  [on_device(): pl.pallas_call(lambda *refs: spread_kernel(plan, *refs), out_shape=jax.Sh...]
    pallas_call x1, Pallas kernels: 1.68 us -> 0.78 us  [on_device(): pl.pallas_call(lambda *refs: finish_kernel(plan, points * devices, *refs)...]
where the time goes in v4:
time: 61 us; the launch traced here: 60.7 us
  blocking collectives  51.5 us (84%)
  Pallas kernels  6.46 us (11%)
  local copies, waits for them, and re-layouts  2.06 us (3%)
  between operations  0.68 us (1%)
    all_to_all x2, blocking collectives, exchanged(): lax.all_to_all(blocks, ROW_COL, split_axis=0, concat_axis=0, tiled=True)  51.5 us
    pallas_call x1, Pallas kernels, on_device(): pl.pallas_call(lambda *refs: tile_kernel(plan, *refs), out_shape=jax.Shap...  5.39 us
    unnamed x10, local copies, waits for them, and re-layouts  2.06 us

profile of v4, /device:TPU:1, one launch (start us, length us, event | category | flops | bytes accessed | tf_op | source)
XLA Modules:
  0.0 60.7 jit_solution(15711989779184982624)
XLA Ops:
  0.6 0.0 copy-start.2
  0.6 0.0 copy-start.3
  0.7 0.0 copy-start.4
  0.7 0.6 %copy-done.2 = f32[128]{0:T(128)S(1)} copy-done((f32[128]{0:T(128)S(1)}, f32[128]{0:T(128)}, u32[]{:S(2)}) %copy-start.2) | copy-done | bytes 536
  1.3 0.0 copy-done.3
  1.3 0.0 copy-done.4
  1.3 0.0 copy-start
  1.3 0.7 %copy-done = f32[16,128]{1,0:T(8,128)S(1)} copy-done((f32[16,128]{1,0:T(8,128)S(1)}, f32[16,128]{1,0:T(8,128)}, u32[]{:S(2)}) %copy-start) | copy-done | bytes 8216
  2.0 0.0 copy-start.1
  2.0 0.7 %copy-done.1 = f32[16,128]{1,0:T(8,128)S(1)} copy-done((f32[16,128]{1,0:T(8,128)S(1)}, f32[16,128]{1,0:T(8,128)}, u32[]{:S(2)}) %copy-start.1) | copy-done | bytes 8216
  2.7 0.3 spread.1
  3.0 32.9 %all_to_all.10 = f32[256,1,384]{2,1,0:T(1,128)S(1)} all-to-all(f32[256,1,384]{2,1,0:T(1,128)S(1)} %bitcast.12), channel_id=1, replica_groups=mesh['row_0'=4,'row_1'=2,'col_0'=8,'col_1'=4] {'row_0','row_1','col_0','..., dimensions={0} | all-to-all | bytes 786432 | tf_op jit(solution)/shard_map/all_to_all | solution.py:181
  35.9 5.4 %tile.1 = f32[256,128]{1,0:T(8,128)S(1)} custom-call(f32[768,128]{1,0:T(8,128)S(1)} %bitcast.11), custom_call_target="tpu_custom_call" | custom-call | tf_op jit(solution)/shard_map/tile/pallas_call | solution.py:194
  41.3 18.6 %all_to_all.11 = f32[256,1,128]{2,1,0:T(1,128)S(1)} all-to-all(f32[256,1,128]{2,1,0:T(1,128)S(1)} %bitcast.14), channel_id=1, replica_groups=mesh['row_0'=4,'row_1'=2,'col_0'=8,'col_1'=4] {'row_0','row_1','col_0','..., dimensions={0} | all-to-all | bytes 262144 | tf_op jit(solution)/shard_map/all_to_all | solution.py:181
  59.9 0.8 %finish.1 = (f32[16,128]{1,0:T(8,128)}, f32[1,128]{1,0:T(1,128)}, f32[1,16]{1,0:T(1,128)}) custom-call(f32[256,128]{1,0:T(8,128)S(1)} %bitcast.13), custom_call_target="tpu_custom_call" | custom-call | tf_op jit(solution)/shard_map/finish/pallas_call | solution.py:210
Async XLA Ops:
  0.6 0.7 %copy-start.2 = (f32[128]{0:T(128)S(1)}, f32[128]{0:T(128)}, u32[]{:S(2)}) copy-start(f32[128]{0:T(128)} %param.6) | copy-start | bytes 1540
  0.6 0.7 %copy-start.3 = (f32[128]{0:T(128)S(1)}, f32[128]{0:T(128)}, u32[]{:S(2)}) copy-start(f32[128]{0:T(128)} %param.8) | copy-start | bytes 1540
  0.7 0.7 %copy-start.4 = (f32[16]{0:T(128)S(1)}, f32[16]{0:T(128)}, u32[]{:S(2)}) copy-start(f32[16]{0:T(128)} %param.9) | copy-start | bytes 196
  1.3 0.7 %copy-start = (f32[16,128]{1,0:T(8,128)S(1)}, f32[16,128]{1,0:T(8,128)}, u32[]{:S(2)}) copy-start(f32[16,128]{1,0:T(8,128)} %refs_0_.1) | copy-start | bytes 24580
  2.0 0.7 %copy-start.1 = (f32[16,128]{1,0:T(8,128)S(1)}, f32[16,128]{1,0:T(8,128)}, u32[]{:S(2)}) copy-start(f32[16,128]{1,0:T(8,128)} %refs_2_.1) | copy-start | bytes 24580

commit v5 on v4

v5 whole, which is shorter than its diff:
```python
import math

import jax
import jax.numpy as jnp
from jax import lax
from jax.experimental import pallas as pl
from jax.experimental.pallas import tpu as pltpu
from jax.sharding import Mesh
from jax.sharding import PartitionSpec as P

CORE = "row_1"
CHIPS = ("row_0", "col_0", "col_1")
CORE_CHIPS = (CORE, *CHIPS)
ROW_COL = ("row_0", "row_1", "col_0", "col_1")
COL_ROW = ("col_0", "col_1", "row_0", "row_1")
LOG2E = math.log2(math.e)
LANES = 128
COL_CLASSES = 8
STEP = 1024
OWN_STEP = 1024
ROW_TILE = 256


def split3(x):
    high = x.astype(jnp.bfloat16).astype(jnp.float32)
    rest = x - high
    middle = rest.astype(jnp.bfloat16).astype(jnp.float32)
    return high, middle, rest - middle


def placed_rows(entries, height, lanes):
    row = lax.broadcasted_iota(jnp.int32, (height, lanes), 0)
    block = jnp.zeros((height, lanes), jnp.float32)
    for k, entry in enumerate(entries):
        block = jnp.where(row == k, entry, block)
    return block


def to_left(x, lanes):
    return pltpu.roll(x, (LANES - lanes) % LANES, 1)


def to_right(x, lanes):
    return pltpu.roll(x, lanes % LANES, 1)


class Plan:
    def __init__(self, chips, dims, points):
        self.chips, self.devices, self.dims = chips, 2 * chips, dims
        self.cols = COL_CLASSES
        self.half = chips // self.cols
        self.rows = 2 * self.half
        self.row_each = points // self.rows
        self.col_each = points // self.cols
        self.of_rows = self.row_each * dims
        self.at_cols = 2 * self.of_rows
        self.at_col_alpha = self.at_cols + self.col_each * dims
        self.at_row_alpha = self.at_col_alpha + self.col_each
        self.tiles = pl.cdiv(self.at_row_alpha + 2 * self.row_each, LANES)
        self.at_weight = self.row_each * dims
        self.at_grad = self.at_weight + pl.cdiv(self.row_each, 8) * 8


def spread_kernel(plan, *refs):
    dims = plan.dims
    sources, out_ref, arrived, sems = refs[:5], refs[5], refs[6:11], refs[11]
    loads = [pltpu.make_async_copy(src, dst, sems.at[k]) for k, (src, dst) in enumerate(zip(sources, arrived))]
    for load in loads:
        load.start()
    for load in loads:
        load.wait()
    rows_ref, row_alpha_ref, cols_ref, col_alpha_ref, scale_ref = arrived
    scales = jnp.broadcast_to(scale_ref[:, :dims], (dims, dims))
    down = lax.broadcasted_iota(jnp.int32, (dims, dims), 0)
    along = lax.broadcasted_iota(jnp.int32, (dims, dims), 1)
    inverse = 1.0 / jnp.sum(jnp.where(down == along, scales, 0.0), 1, keepdims=True)
    rows = rows_ref[...] * inverse
    cols = cols_ref[...] * inverse
    of_class = [c * plan.half + i * plan.rows for c in range(2) for i in range(plan.row_each)]
    of_col = [i * plan.cols for i in range(plan.col_each)]
    pieces = [to_left(rows, k) for k in of_class] + [to_left(cols, k) for k in of_col]
    alphas = [to_left(col_alpha_ref[...], k) for k in of_col] + [to_left(row_alpha_ref[...], k) for k in of_class]
    pieces.append(placed_rows(alphas, plan.tiles * LANES - plan.at_col_alpha, LANES))
    stacked = jnp.concatenate(pieces, 0)
    for k in range(plan.tiles):
        turned = stacked[k * LANES:(k + 1) * LANES].T
        lane = lax.broadcasted_iota(jnp.int32, (plan.cols, LANES), 1) + k * LANES
        is_row = (lane < plan.at_cols) | (lane >= plan.at_row_alpha)
        of_cols = turned[:plan.cols]
        for r in range(plan.half):
            of_row = jnp.broadcast_to(turned[r:r + 1], (plan.cols, LANES))
            start = r * plan.cols * plan.tiles + k
            out_ref[pl.ds(start, plan.cols, stride=plan.tiles), :] = jnp.where(is_row, of_row, of_cols)


def prepared_exponents(unit, ones_first):
    dims, width = unit.shape
    scaled = unit * math.sqrt(LOG2E)
    norm = -0.5 * jnp.sum(scaled * scaled, 0, keepdims=True)
    parts = split3(norm)
    ones = (1.0, 1.0, 1.0)
    norms = placed_rows(ones + parts if ones_first else parts + ones, dims, width)
    h, m, l = split3(scaled)
    if ones_first:
        return h, m, h, m, l, h, norms, jnp.zeros_like(norms)
    return h, h, m, m, h, l, norms, jnp.zeros_like(norms)


def prepare(plan, in_ref, t_ref, b_ref, v_ref, a_ref):
    dims, width = plan.dims, plan.chips
    bf16 = jnp.bfloat16
    core = lax.axis_index(CORE)
    for k in range(plan.tiles):
        t_ref[k * LANES:(k + 1) * LANES, :] = in_ref[pl.ds(k, width, stride=plan.tiles), :].T
    for i in range(plan.row_each):
        unit = t_ref[pl.ds(pl.multiple_of(core * plan.of_rows, 8) + i * dims, dims), :]
        for g, block in enumerate(prepared_exponents(unit, False)):
            a_ref[g * dims:(g + 1) * dims, i * width:(i + 1) * width] = block.astype(bf16)
    for i in range(plan.col_each):
        at = plan.at_cols + i * dims
        unit = t_ref[at:at + dims, :]
        alpha = t_ref[plan.at_col_alpha + i:plan.at_col_alpha + i + 1, :]
        b_ref[i * width:(i + 1) * width, :] = jnp.concatenate(prepared_exponents(unit, True), 0).astype(bf16).T
        weighted = alpha * unit
        fh, fm, fl = split3(weighted)
        sh, sm, sl = split3(weighted * unit)
        alphas = placed_rows(split3(alpha), dims, width)
        for g, block in enumerate((fh, fm, sh, sm, alphas, fl, sl)):
            v_ref[g * dims:(g + 1) * dims, i * width:(i + 1) * width] = block.astype(bf16)


def add_columns(plan, sums, a_tiles, b_ref, v_ref, step):
    f32, bf16 = jnp.float32, jnp.bfloat16
    sums = list(sums)
    for start in range(0, b_ref.shape[0], step):
        points = b_ref[start:start + step, :]
        values = v_ref[:, start:start + step]
        kernels = [jnp.exp2(jnp.dot(points, a_tile, preferred_element_type=f32)) for a_tile in a_tiles]
        highs = [kernel.astype(bf16) for kernel in kernels]
        lows = [(kernel - high.astype(f32)).astype(bf16) for kernel, high in zip(kernels, highs)]
        bigs = [jnp.dot(values, high, preferred_element_type=f32) for high in highs]
        smalls = [jnp.dot(values[:5 * plan.dims], low, preferred_element_type=f32) for low in lows]
        sums = [(s[0] + big, s[1] + small) for s, big, small in zip(sums, bigs, smalls)]
    return sums


def zero_sums(plan):
    return jnp.zeros((7 * plan.dims, ROW_TILE), jnp.float32), jnp.zeros((5 * plan.dims, ROW_TILE), jnp.float32)


def own_kernel(plan, own_ref, t_ref, b_ref, v_ref, a_ref, big_ref, small_ref):
    prepare(plan, own_ref, t_ref, b_ref, v_ref, a_ref)
    cuts = row_cuts(a_ref)
    sums = add_columns(plan, [zero_sums(plan)] * len(cuts), [a_ref[:, cut] for cut in cuts], b_ref, v_ref, OWN_STEP)
    for cut, (big, small) in zip(cuts, sums):
        big_ref[:, cut], small_ref[:, cut] = big, small


def row_cuts(a_ref):
    return [slice(start, start + ROW_TILE) for start in range(0, a_ref.shape[1], ROW_TILE)]


def tile_kernel(plan, other_ref, own_t_ref, own_b_ref, own_v_ref, own_a_ref, big_ref, small_ref, out_ref, t_ref, b_ref, v_ref, a_ref, o_ref):
    dims, width = plan.dims, plan.chips
    prepare(plan, other_ref, t_ref, b_ref, v_ref, a_ref)
    core = lax.axis_index(CORE)
    grad = jnp.zeros((dims, width), jnp.float32)
    o_ref[plan.at_weight:, :] = jnp.zeros((LANES - plan.at_weight, 2 * width), jnp.float32)
    for points_ref, rows_ref, place in ((own_t_ref, own_a_ref, core), (t_ref, a_ref, 1 - core)):
        lanes = pl.ds(pl.multiple_of(place * width, LANES), width)
        cuts = row_cuts(rows_ref)
        a_tiles = [rows_ref[:, cut] for cut in cuts]
        if rows_ref is own_a_ref:
            sums = [(big_ref[:, cut], small_ref[:, cut]) for cut in cuts]
        else:
            sums = add_columns(plan, [zero_sums(plan)] * len(cuts), a_tiles, own_b_ref, own_v_ref, STEP)
        sums = add_columns(plan, sums, a_tiles, b_ref, v_ref, STEP)
        for cut, (big, small) in zip(cuts, sums):
            start = cut.start

            def part(x, g):
                return x[g * dims:(g + 1) * dims]

            first = (part(small, 0) + part(small, 1) + part(big, 5)) + part(big, 1) + part(big, 0)
            second = (part(small, 2) + part(small, 3) + part(big, 6)) + part(big, 3) + part(big, 2)
            weights = part(big, 4) + part(small, 4)
            weight = weights[0:1] + weights[1:2] + weights[2:3]
            for i in range(start // width, (start + ROW_TILE) // width):
                cut = slice(i * width - start, (i + 1) * width - start)
                unit = points_ref[pl.ds(pl.multiple_of(core * plan.of_rows, 8) + i * dims, dims), :]
                alpha = points_ref[pl.ds(plan.at_row_alpha + core * plan.row_each + i, 1), :]
                terms = 0.5 * alpha * (unit * unit * weight[:, cut] - 2.0 * unit * first[:, cut] + second[:, cut])
                o_ref[i * dims:(i + 1) * dims, lanes] = terms
                o_ref[plan.at_weight + i:plan.at_weight + i + 1, lanes] = weight[:, cut]
                grad = grad + terms
    share = jnp.sum(grad, 1, keepdims=True)
    o_ref[plan.at_grad:plan.at_grad + dims, :] = jnp.broadcast_to(share, (dims, 2 * width))
    out_ref[...] = o_ref[...].T


def finish_kernel(plan, total_rows, in_ref, terms_ref, weight_ref, grad_ref):
    dims = plan.dims
    summed = jnp.sum(in_ref[...].reshape(plan.rows, plan.cols, LANES), 1)
    total = jnp.sum(summed, 0, keepdims=True)
    padded = jnp.concatenate([summed, jnp.zeros((LANES - plan.rows, LANES), jnp.float32)], 0)
    turned = padded.T
    terms = turned[:dims]
    weight = turned[plan.at_weight:plan.at_weight + 1]
    for i in range(1, plan.row_each):
        terms = terms + to_right(turned[i * dims:(i + 1) * dims], i * plan.rows)
        weight = weight + to_right(turned[plan.at_weight + i:plan.at_weight + i + 1], i * plan.rows)
    terms_ref[...] = terms
    weight_ref[...] = weight
    grad_ref[...] = to_left(total, plan.at_grad)[:, :dims] / total_rows


def on_device(x_rows, alpha_rows, x_cols, alpha_cols, lengthscale):
    dims, points = x_rows.shape
    chips = lax.axis_size(CHIPS)
    devices = 2 * chips
    plan = Plan(chips, dims, points)
    whole = pl.BlockSpec(memory_space=pltpu.VMEM)
    f32, bf16 = jnp.float32, jnp.bfloat16

    def exchanged(x, axes):
        blocks = x.reshape(lax.axis_size(axes), 1, -1)
        return lax.all_to_all(blocks, axes, split_axis=0, concat_axis=0, tiled=True).reshape(x.shape)

    sources = (x_rows, alpha_rows.reshape(1, points), x_cols, alpha_cols.reshape(1, points), lengthscale.reshape(1, dims))
    blocks = pl.pallas_call(
        lambda *refs: spread_kernel(plan, *refs),
        out_shape=jax.ShapeDtypeStruct((chips * plan.tiles, LANES), f32),
        in_specs=[pl.BlockSpec(memory_space=pltpu.HBM)] * 5,
        out_specs=whole,
        scratch_shapes=[
            pltpu.VMEM((dims, points), f32),
            pltpu.VMEM((1, points), f32),
            pltpu.VMEM((dims, points), f32),
            pltpu.VMEM((1, points), f32),
            pltpu.VMEM((1, dims), f32),
            pltpu.SemaphoreType.DMA((5,)),
        ],
        compiler_params=pltpu.CompilerParams(vmem_limit_bytes=4 << 20),
        name="spread",
    )(*(pltpu.with_memory_space_constraint(x, pltpu.HBM) for x in sources))
    own = exchanged(blocks, CHIPS)
    other = lax.ppermute(own, CORE, [(0, 1), (1, 0)])
    row_half, col_half = plan.row_each * chips, plan.col_each * chips
    prepared = (
        jax.ShapeDtypeStruct((plan.tiles * LANES, chips), f32),
        jax.ShapeDtypeStruct((col_half, 8 * dims), bf16),
        jax.ShapeDtypeStruct((7 * dims, col_half), bf16),
        jax.ShapeDtypeStruct((8 * dims, row_half), bf16),
    )
    sums = (
        jax.ShapeDtypeStruct((7 * dims, row_half), f32),
        jax.ShapeDtypeStruct((5 * dims, row_half), f32),
    )
    own_parts = pl.pallas_call(
        lambda *refs: own_kernel(plan, *refs),
        out_shape=prepared + sums,
        in_specs=[whole],
        out_specs=(whole,) * 6,
        compiler_params=pltpu.CompilerParams(vmem_limit_bytes=12 << 20),
        cost_estimate=pl.CostEstimate(flops=2 << 30, bytes_accessed=1 << 20, transcendentals=0),
        name="own",
    )(own)
    shares = pl.pallas_call(
        lambda *refs: tile_kernel(plan, *refs),
        out_shape=jax.ShapeDtypeStruct((devices, LANES), f32),
        in_specs=[whole] * 7,
        out_specs=whole,
        scratch_shapes=[
            *(pltpu.VMEM(part.shape, part.dtype) for part in prepared),
            pltpu.VMEM((LANES, devices), f32),
        ],
        compiler_params=pltpu.CompilerParams(vmem_limit_bytes=16 << 20),
        name="tile",
    )(other, *own_parts)
    arrived = exchanged(shares, CORE_CHIPS)
    terms, weight, grad = pl.pallas_call(
        lambda *refs: finish_kernel(plan, points * devices, *refs),
        out_shape=(
            jax.ShapeDtypeStruct((dims, points), f32),
            jax.ShapeDtypeStruct((1, points), f32),
            jax.ShapeDtypeStruct((1, dims), f32),
        ),
        in_specs=[whole],
        out_specs=(whole, whole, whole),
        compiler_params=pltpu.CompilerParams(vmem_limit_bytes=4 << 20),
        name="finish",
    )(arrived)
    return terms, weight.reshape(points), grad.reshape(dims)


def solution(mesh):
    finer = Mesh(mesh.devices.reshape(4, 2, 8, 4), ROW_COL)
    in_specs = (P(None, ROW_COL), P(ROW_COL), P(None, COL_ROW), P(COL_ROW), P())
    out_specs = (P(None, ROW_COL), P(ROW_COL), P())
    return jax.shard_map(on_device, mesh=finer, in_specs=in_specs, out_specs=out_specs, check_vma=False)
```

time: 61 us -> 57.9 us (0.949)
  blocking collectives: 51.5 us -> 46.4 us
  starting transfers between devices: 0 us -> 3.02 us
  local copies, waits for them, and re-layouts: 2.06 us -> 0 us
  Pallas kernels: 6.46 us -> 7.64 us
    all_to_all x2, blocking collectives: 51.5 us -> 46.4 us  [exchanged(): lax.all_to_all(blocks, axes, split_axis=0, concat_axis=0, tiled=True)]
    ppermute x0 -> x1, starting transfers between devices: none -> 3.02 us  [on_device(): other = lax.ppermute(own, CORE, [(0, 1), (1, 0)])]
    unnamed x10 -> x0, local copies, waits for them, and re-layouts: 2.06 us -> none
    pallas_call x0 -> x1, Pallas kernels: none -> 1.73 us  [on_device(): pl.pallas_call(lambda *refs: own_kernel(plan, *refs), out_shape=prepared...]
    pallas_call x1, Pallas kernels: 5.39 us -> 4.06 us  [on_device(): pl.pallas_call(lambda *refs: tile_kernel(plan, *refs), out_shape=jax.Shap...]
    pallas_call x1, Pallas kernels: 0.29 us -> 1.07 us  [on_device(): pl.pallas_call(lambda *refs: spread_kernel(plan, *refs), out_shape=jax.Sh...]
  transfers between devices with their start and end apart: 0 -> 1, of which waited for: 0 -> 0; matrix products, arithmetic and copies ran while one was open for 0% -> 0% of each run, Pallas kernels for 0% -> 3%
where the time goes in v5:
time: 57.9 us; the launch traced here: 57.7 us
  blocking collectives  46.4 us (80%)
  Pallas kernels  7.64 us (13%)
  starting transfers between devices  3.02 us (5%)
  between operations  0.65 us (1%)
    all_to_all x2, blocking collectives, exchanged(): lax.all_to_all(blocks, axes, split_axis=0, concat_axis=0, tiled=True)  46.4 us
    pallas_call x1, Pallas kernels, on_device(): pl.pallas_call(lambda *refs: tile_kernel(plan, *refs), out_shape=jax.Shap...  4.06 us
    ppermute x1, starting transfers between devices, on_device(): other = lax.ppermute(own, CORE, [(0, 1), (1, 0)])  3.02 us
    pallas_call x1, Pallas kernels, on_device(): pl.pallas_call(lambda *refs: own_kernel(plan, *refs), out_shape=prepared...  1.73 us
  transfers between devices with their start and end apart: 1, of which 0 were waited for; matrix products, arithmetic and copies ran while one was open for 0% of the time, Pallas kernels for 3%

profile of v5, /device:TPU:1, one launch (start us, length us, event | category | flops | bytes accessed | tf_op | source)
XLA Modules:
  0.0 57.7 jit_solution(7935366017312593822)
XLA Ops:
  0.6 1.1 %spread.1 = f32[512,128]{1,0:T(8,128)S(1)} custom-call(f32[16,128]{1,0:T(8,128)} %refs_0_.1, f32[1,128]{1,0:T(1,128)} %bitcast.16, f32[16,128]{1,0:T(8,128)} %refs_2_.1, f32[1,128]{1,0:T(1,128)} %bitcast.17, f32[1,16]{1,0:T(1,128)} %bitcast.18), custom_call_target="tpu_custom_call" | custom-call | tf_op jit(solution)/shard_map/spread/pallas_call | solution.py:230
  1.7 28.6 %all_to_all.10 = f32[128,1,512]{2,1,0:T(1,128)S(1)} all-to-all(f32[128,1,512]{2,1,0:T(1,128)S(1)} %bitcast.11), channel_id=1, replica_groups=mesh['row_0'=4,'row_1'=2,'col_0'=8,'col_1'=4] {'row_0','col_0','col_1'}, dimensions={0} | all-to-all | bytes 524288 | tf_op jit(solution)/shard_map/all_to_all | solution.py:227
  30.3 3.0 %collective-permute-start = (f32[512,128]{1,0:T(8,128)S(1)}, f32[512,128]{1,0:T(8,128)S(1)}, u32[]{:S(2)}, u32[]{:S(2)}) collective-permute-start(f32[512,128]{1,0:T(8,128)S(1)} %bitcast.14), channel_id=1, source_target_pairs={{0,32},{32,0},{1,33},{33,1},{2,34},{34,2},{3,35},{35,3},{4,36},{36... | collective-permute-start | bytes 786440 | tf_op jit(solution)/shard_map/ppermute | solution.py:247
  33.4 1.7 %own.1 = (f32[512,128]{1,0:T(8,128)S(1)}, bf16[2048,128]{1,0:T(8,128)(2,1)S(1)}, bf16[112,2048]{1,0:T(8,128)(2,1)S(1)}, bf16[128,512]{1,0:T(8,128)(2,1)S(1)}, f3...) custom-call(f32[512,128]{1,0:T(8,128)S(1)} %bitcast.15), custom_call_target="tpu_custom_call" | custom-call | flops 2147483648 | bytes 1048576 | tf_op jit(solution)/shard_map/own/pallas_call | solution.py:259
  35.1 0.0 collective-permute-done.refs_0_
  35.1 4.1 %tile.1 = f32[256,128]{1,0:T(8,128)S(1)} custom-call(f32[512,128]{1,0:T(8,128)S(1)} %collective-permute-done.refs_0_, f32[512,128]{1,0:T(8,128)S(1)} %get-tuple-element.12.refs_1_, bf16[2048,128]{1,0:T(8,128)(2,1)S(1)} %get-tuple-element.13.refs_2_, bf16[112,2048]{1,0:T(8,128)(2,1)S(1)} %get-tuple-element.14.refs_3_, ...), custom_call_target="tpu_custom_call" | custom-call | tf_op jit(solution)/shard_map/tile/pallas_call | solution.py:268
  39.2 17.7 %all_to_all.11 = f32[256,1,128]{2,1,0:T(1,128)S(1)} all-to-all(f32[256,1,128]{2,1,0:T(1,128)S(1)} %bitcast.12), channel_id=1, replica_groups=mesh['row_0'=4,'row_1'=2,'col_0'=8,'col_1'=4] {'row_1','row_0','col_0','..., dimensions={0} | all-to-all | bytes 262144 | tf_op jit(solution)/shard_map/all_to_all | solution.py:227
  56.9 0.8 %finish.1 = (f32[16,128]{1,0:T(8,128)}, f32[1,128]{1,0:T(1,128)}, f32[1,16]{1,0:T(1,128)}) custom-call(f32[256,128]{1,0:T(8,128)S(1)} %bitcast.13), custom_call_target="tpu_custom_call" | custom-call | tf_op jit(solution)/shard_map/finish/pallas_call | solution.py:281
Async XLA Ops:
  30.3 4.8 %collective-permute-start = (f32[512,128]{1,0:T(8,128)S(1)}, f32[512,128]{1,0:T(8,128)S(1)}, u32[]{:S(2)}, u32[]{:S(2)}) collective-permute-start(f32[512,128]{1,0:T(8,128)S(1)} %bitcast.14), channel_id=1, source_target_pairs={{0,32},{32,0},{1,33},{33,1},{2,34},{34,2},{3,35},{35,3},{4,36},{36... | collective-permute-start | bytes 786440 | tf_op jit(solution)/shard_map/ppermute | solution.py:247

commit v6 on v5

--- a/solution.py
+++ b/solution.py
@@ -10,7 +10,7 @@
 
 CORE = "row_1"
 CHIPS = ("row_0", "col_0", "col_1")
-CORE_CHIPS = (CORE, *CHIPS)
+CHIPS_CORE = (*CHIPS, CORE)
 ROW_COL = ("row_0", "row_1", "col_0", "col_1")
 COL_ROW = ("col_0", "col_1", "row_0", "row_1")
 LOG2E = math.log2(math.e)
@@ -106,7 +106,7 @@
     return h, h, m, m, h, l, norms, jnp.zeros_like(norms)
 
 
-def prepare(plan, in_ref, t_ref, b_ref, v_ref, a_ref):
+def prepare_rows(plan, in_ref, t_ref, a_ref):
     dims, width = plan.dims, plan.chips
     bf16 = jnp.bfloat16
     core = lax.axis_index(CORE)
@@ -116,6 +116,11 @@
         unit = t_ref[pl.ds(pl.multiple_of(core * plan.of_rows, 8) + i * dims, dims), :]
         for g, block in enumerate(prepared_exponents(unit, False)):
             a_ref[g * dims:(g + 1) * dims, i * width:(i + 1) * width] = block.astype(bf16)
+
+
+def prepare_cols(plan, t_ref, b_ref, v_ref):
+    dims, width = plan.dims, plan.chips
+    bf16 = jnp.bfloat16
     for i in range(plan.col_each):
         at = plan.at_cols + i * dims
         unit = t_ref[at:at + dims, :]
@@ -149,10 +154,11 @@
 
 
 def own_kernel(plan, own_ref, t_ref, b_ref, v_ref, a_ref, big_ref, small_ref):
-    prepare(plan, own_ref, t_ref, b_ref, v_ref, a_ref)
+    prepare_rows(plan, own_ref, t_ref, a_ref)
+    prepare_cols(plan, t_ref, b_ref, v_ref)
     cuts = row_cuts(a_ref)
-    sums = add_columns(plan, [zero_sums(plan)] * len(cuts), [a_ref[:, cut] for cut in cuts], b_ref, v_ref, OWN_STEP)
-    for cut, (big, small) in zip(cuts, sums):
+    for cut in cuts:
+        (big, small), = add_columns(plan, [zero_sums(plan)], [a_ref[:, cut]], b_ref, v_ref, OWN_STEP)
         big_ref[:, cut], small_ref[:, cut] = big, small
 
 
@@ -162,7 +168,10 @@
 
 def tile_kernel(plan, other_ref, own_t_ref, own_b_ref, own_v_ref, own_a_ref, big_ref, small_ref, out_ref, t_ref, b_ref, v_ref, a_ref, o_ref):
     dims, width = plan.dims, plan.chips
-    prepare(plan, other_ref, t_ref, b_ref, v_ref, a_ref)
+    prepare_rows(plan, other_ref, t_ref, a_ref)
+    cuts = row_cuts(a_ref)
+    other_sums = add_columns(plan, [zero_sums(plan)] * len(cuts), [a_ref[:, cut] for cut in cuts], own_b_ref, own_v_ref, STEP)
+    prepare_cols(plan, t_ref, b_ref, v_ref)
     core = lax.axis_index(CORE)
     grad = jnp.zeros((dims, width), jnp.float32)
     o_ref[plan.at_weight:, :] = jnp.zeros((LANES - plan.at_weight, 2 * width), jnp.float32)
@@ -173,7 +182,7 @@
         if rows_ref is own_a_ref:
             sums = [(big_ref[:, cut], small_ref[:, cut]) for cut in cuts]
         else:
-            sums = add_columns(plan, [zero_sums(plan)] * len(cuts), a_tiles, own_b_ref, own_v_ref, STEP)
+            sums = other_sums
         sums = add_columns(plan, sums, a_tiles, b_ref, v_ref, STEP)
         for cut, (big, small) in zip(cuts, sums):
             start = cut.start
@@ -195,12 +204,14 @@
                 grad = grad + terms
     share = jnp.sum(grad, 1, keepdims=True)
     o_ref[plan.at_grad:plan.at_grad + dims, :] = jnp.broadcast_to(share, (dims, 2 * width))
-    out_ref[...] = o_ref[...].T
+    for place in range(2):
+        out_ref[pl.ds(place, width, stride=2), :] = o_ref[:, place * width:(place + 1) * width].T
 
 
 def finish_kernel(plan, total_rows, in_ref, terms_ref, weight_ref, grad_ref):
     dims = plan.dims
-    summed = jnp.sum(in_ref[...].reshape(plan.rows, plan.cols, LANES), 1)
+    by_core = [in_ref[pl.ds(core, plan.chips, stride=2), :] for core in range(2)]
+    summed = jnp.concatenate([jnp.sum(x.reshape(plan.half, plan.cols, LANES), 1) for x in by_core], 0)
     total = jnp.sum(summed, 0, keepdims=True)
     padded = jnp.concatenate([summed, jnp.zeros((LANES - plan.rows, LANES), jnp.float32)], 0)
     turned = padded.T
@@ -277,7 +288,7 @@
         compiler_params=pltpu.CompilerParams(vmem_limit_bytes=16 << 20),
         name="tile",
     )(other, *own_parts)
-    arrived = exchanged(shares, CORE_CHIPS)
+    arrived = exchanged(shares, CHIPS_CORE)
     terms, weight, grad = pl.pallas_call(
         lambda *refs: finish_kernel(plan, points * devices, *refs),
         out_shape=(

time: 57.9 us -> 57.6 us (level)
  no operation moved by 1% of the time
where the time goes in v6:
time: 57.6 us; the launch traced here: 57.4 us
  blocking collectives  46.3 us (80%)
  Pallas kernels  7.39 us (13%)
  starting transfers between devices  3.02 us (5%)
  between operations  0.66 us (1%)
    all_to_all x2, blocking collectives, exchanged(): lax.all_to_all(blocks, axes, split_axis=0, concat_axis=0, tiled=True)  46.3 us
    pallas_call x1, Pallas kernels, on_device(): pl.pallas_call(lambda *refs: tile_kernel(plan, *refs), out_shape=jax.Shap...  3.89 us
    ppermute x1, starting transfers between devices, on_device(): other = lax.ppermute(own, CORE, [(0, 1), (1, 0)])  3.02 us
    pallas_call x1, Pallas kernels, on_device(): pl.pallas_call(lambda *refs: own_kernel(plan, *refs), out_shape=prepared...  1.65 us
  transfers between devices with their start and end apart: 1, of which 0 were waited for; matrix products, arithmetic and copies ran while one was open for 0% of the time, Pallas kernels for 3%

profile of v6, /device:TPU:1, one launch (start us, length us, event | category | flops | bytes accessed | tf_op | source)
XLA Modules:
  0.0 57.4 jit_solution(3613773959337391117)
XLA Ops:
  0.6 1.1 %spread.1 = f32[512,128]{1,0:T(8,128)S(1)} custom-call(f32[16,128]{1,0:T(8,128)} %refs_0_.1, f32[1,128]{1,0:T(1,128)} %bitcast.16, f32[16,128]{1,0:T(8,128)} %refs_2_.1, f32[1,128]{1,0:T(1,128)} %bitcast.17, f32[1,16]{1,0:T(1,128)} %bitcast.18), custom_call_target="tpu_custom_call" | custom-call | tf_op jit(solution)/shard_map/spread/pallas_call | solution.py:241
  1.7 28.6 %all_to_all.10 = f32[128,1,512]{2,1,0:T(1,128)S(1)} all-to-all(f32[128,1,512]{2,1,0:T(1,128)S(1)} %bitcast.11), channel_id=1, replica_groups=mesh['row_0'=4,'row_1'=2,'col_0'=8,'col_1'=4] {'row_0','col_0','col_1'}, dimensions={0} | all-to-all | bytes 524288 | tf_op jit(solution)/shard_map/all_to_all | solution.py:238
  30.3 3.0 %collective-permute-start = (f32[512,128]{1,0:T(8,128)S(1)}, f32[512,128]{1,0:T(8,128)S(1)}, u32[]{:S(2)}, u32[]{:S(2)}) collective-permute-start(f32[512,128]{1,0:T(8,128)S(1)} %bitcast.14), channel_id=1, source_target_pairs={{0,32},{32,0},{1,33},{33,1},{2,34},{34,2},{3,35},{35,3},{4,36},{36... | collective-permute-start | bytes 786440 | tf_op jit(solution)/shard_map/ppermute | solution.py:258
  33.4 1.6 %own.1 = (f32[512,128]{1,0:T(8,128)S(1)}, bf16[2048,128]{1,0:T(8,128)(2,1)S(1)}, bf16[112,2048]{1,0:T(8,128)(2,1)S(1)}, bf16[128,512]{1,0:T(8,128)(2,1)S(1)}, f3...) custom-call(f32[512,128]{1,0:T(8,128)S(1)} %bitcast.15), custom_call_target="tpu_custom_call" | custom-call | flops 2147483648 | bytes 1048576 | tf_op jit(solution)/shard_map/own/pallas_call | solution.py:270
  35.0 0.0 collective-permute-done.refs_0_
  35.0 3.9 %tile.1 = f32[256,128]{1,0:T(8,128)S(1)} custom-call(f32[512,128]{1,0:T(8,128)S(1)} %collective-permute-done.refs_0_, f32[512,128]{1,0:T(8,128)S(1)} %get-tuple-element.12.refs_1_, bf16[2048,128]{1,0:T(8,128)(2,1)S(1)} %get-tuple-element.13.refs_2_, bf16[112,2048]{1,0:T(8,128)(2,1)S(1)} %get-tuple-element.14.refs_3_, ...), custom_call_target="tpu_custom_call" | custom-call | tf_op jit(solution)/shard_map/tile/pallas_call | solution.py:279
  38.9 17.7 %all_to_all.11 = f32[256,1,128]{2,1,0:T(1,128)S(1)} all-to-all(f32[256,1,128]{2,1,0:T(1,128)S(1)} %bitcast.12), channel_id=1, replica_groups=mesh['row_0'=4,'row_1'=2,'col_0'=8,'col_1'=4] {'row_0','col_0','col_1','..., dimensions={0} | all-to-all | bytes 262144 | tf_op jit(solution)/shard_map/all_to_all | solution.py:238
  56.6 0.8 %finish.1 = (f32[16,128]{1,0:T(8,128)}, f32[1,128]{1,0:T(1,128)}, f32[1,16]{1,0:T(1,128)}) custom-call(f32[256,128]{1,0:T(8,128)S(1)} %bitcast.13), custom_call_target="tpu_custom_call" | custom-call | tf_op jit(solution)/shard_map/finish/pallas_call | solution.py:292
Async XLA Ops:
  30.3 4.7 %collective-permute-start = (f32[512,128]{1,0:T(8,128)S(1)}, f32[512,128]{1,0:T(8,128)S(1)}, u32[]{:S(2)}, u32[]{:S(2)}) collective-permute-start(f32[512,128]{1,0:T(8,128)S(1)} %bitcast.14), channel_id=1, source_target_pairs={{0,32},{32,0},{1,33},{33,1},{2,34},{34,2},{3,35},{35,3},{4,36},{36... | collective-permute-start | bytes 786440 | tf_op jit(solution)/shard_map/ppermute | solution.py:258

commit v7 on v6

--- a/solution.py
+++ b/solution.py
@@ -17,7 +17,6 @@
 LANES = 128
 COL_CLASSES = 8
 STEP = 1024
-OWN_STEP = 1024
 ROW_TILE = 256
 
 
@@ -158,7 +157,7 @@
     prepare_cols(plan, t_ref, b_ref, v_ref)
     cuts = row_cuts(a_ref)
     for cut in cuts:
-        (big, small), = add_columns(plan, [zero_sums(plan)], [a_ref[:, cut]], b_ref, v_ref, OWN_STEP)
+        (big, small), = add_columns(plan, [zero_sums(plan)], [a_ref[:, cut]], b_ref, v_ref, STEP)
         big_ref[:, cut], small_ref[:, cut] = big, small
 
 
@@ -175,33 +174,28 @@
     core = lax.axis_index(CORE)
     grad = jnp.zeros((dims, width), jnp.float32)
     o_ref[plan.at_weight:, :] = jnp.zeros((LANES - plan.at_weight, 2 * width), jnp.float32)
-    for points_ref, rows_ref, place in ((own_t_ref, own_a_ref, core), (t_ref, a_ref, 1 - core)):
+    tiles = [(own_t_ref, own_a_ref, cut, core) for cut in cuts] + [(t_ref, a_ref, cut, 1 - core) for cut in cuts]
+    sums = [(big_ref[:, cut], small_ref[:, cut]) for cut in cuts] + other_sums
+    sums = add_columns(plan, sums, [rows_ref[:, cut] for _, rows_ref, cut, _ in tiles], b_ref, v_ref, STEP)
+    for (points_ref, _, cut, place), (big, small) in zip(tiles, sums):
         lanes = pl.ds(pl.multiple_of(place * width, LANES), width)
-        cuts = row_cuts(rows_ref)
-        a_tiles = [rows_ref[:, cut] for cut in cuts]
-        if rows_ref is own_a_ref:
-            sums = [(big_ref[:, cut], small_ref[:, cut]) for cut in cuts]
-        else:
-            sums = other_sums
-        sums = add_columns(plan, sums, a_tiles, b_ref, v_ref, STEP)
-        for cut, (big, small) in zip(cuts, sums):
-            start = cut.start
-
-            def part(x, g):
-                return x[g * dims:(g + 1) * dims]
-
-            first = (part(small, 0) + part(small, 1) + part(big, 5)) + part(big, 1) + part(big, 0)
-            second = (part(small, 2) + part(small, 3) + part(big, 6)) + part(big, 3) + part(big, 2)
-            weights = part(big, 4) + part(small, 4)
-            weight = weights[0:1] + weights[1:2] + weights[2:3]
-            for i in range(start // width, (start + ROW_TILE) // width):
-                cut = slice(i * width - start, (i + 1) * width - start)
-                unit = points_ref[pl.ds(pl.multiple_of(core * plan.of_rows, 8) + i * dims, dims), :]
-                alpha = points_ref[pl.ds(plan.at_row_alpha + core * plan.row_each + i, 1), :]
-                terms = 0.5 * alpha * (unit * unit * weight[:, cut] - 2.0 * unit * first[:, cut] + second[:, cut])
-                o_ref[i * dims:(i + 1) * dims, lanes] = terms
-                o_ref[plan.at_weight + i:plan.at_weight + i + 1, lanes] = weight[:, cut]
-                grad = grad + terms
+        start = cut.start
+
+        def part(x, g):
+            return x[g * dims:(g + 1) * dims]
+
+        first = (part(small, 0) + part(small, 1) + part(big, 5)) + part(big, 1) + part(big, 0)
+        second = (part(small, 2) + part(small, 3) + part(big, 6)) + part(big, 3) + part(big, 2)
+        weights = part(big, 4) + part(small, 4)
+        weight = weights[0:1] + weights[1:2] + weights[2:3]
+        for i in range(start // width, (start + ROW_TILE) // width):
+            cut = slice(i * width - start, (i + 1) * width - start)
+            unit = points_ref[pl.ds(pl.multiple_of(core * plan.of_rows, 8) + i * dims, dims), :]
+            alpha = points_ref[pl.ds(plan.at_row_alpha + core * plan.row_each + i, 1), :]
+            terms = 0.5 * alpha * (unit * unit * weight[:, cut] - 2.0 * unit * first[:, cut] + second[:, cut])
+            o_ref[i * dims:(i + 1) * dims, lanes] = terms
+            o_ref[plan.at_weight + i:plan.at_weight + i + 1, lanes] = weight[:, cut]
+            grad = grad + terms
     share = jnp.sum(grad, 1, keepdims=True)
     o_ref[plan.at_grad:plan.at_grad + dims, :] = jnp.broadcast_to(share, (dims, 2 * width))
     for place in range(2):

time: 57.6 us -> 57.5 us (level)
  no operation moved by 1% of the time
where the time goes in v7:
time: 57.5 us; the launch traced here: 57.3 us
  blocking collectives  46.3 us (81%)
  Pallas kernels  7.3 us (13%)
  starting transfers between devices  3.02 us (5%)
  between operations  0.66 us (1%)
    all_to_all x2, blocking collectives, exchanged(): lax.all_to_all(blocks, axes, split_axis=0, concat_axis=0, tiled=True)  46.3 us
    pallas_call x1, Pallas kernels, on_device(): pl.pallas_call(lambda *refs: tile_kernel(plan, *refs), out_shape=jax.Shap...  3.81 us
    ppermute x1, starting transfers between devices, on_device(): other = lax.ppermute(own, CORE, [(0, 1), (1, 0)])  3.02 us
    pallas_call x1, Pallas kernels, on_device(): pl.pallas_call(lambda *refs: own_kernel(plan, *refs), out_shape=prepared...  1.65 us
  transfers between devices with their start and end apart: 1, of which 0 were waited for; matrix products, arithmetic and copies ran while one was open for 0% of the time, Pallas kernels for 3%

profile of v7, /device:TPU:1, one launch (start us, length us, event | category | flops | bytes accessed | tf_op | source)
XLA Modules:
  0.0 57.3 jit_solution(3560084094569872450)
XLA Ops:
  0.6 1.1 %spread.1 = f32[512,128]{1,0:T(8,128)S(1)} custom-call(f32[16,128]{1,0:T(8,128)} %refs_0_.1, f32[1,128]{1,0:T(1,128)} %bitcast.16, f32[16,128]{1,0:T(8,128)} %refs_2_.1, f32[1,128]{1,0:T(1,128)} %bitcast.17, f32[1,16]{1,0:T(1,128)} %bitcast.18), custom_call_target="tpu_custom_call" | custom-call | tf_op jit(solution)/shard_map/spread/pallas_call | solution.py:235
  1.7 28.6 %all_to_all.10 = f32[128,1,512]{2,1,0:T(1,128)S(1)} all-to-all(f32[128,1,512]{2,1,0:T(1,128)S(1)} %bitcast.11), channel_id=1, replica_groups=mesh['row_0'=4,'row_1'=2,'col_0'=8,'col_1'=4] {'row_0','col_0','col_1'}, dimensions={0} | all-to-all | bytes 524288 | tf_op jit(solution)/shard_map/all_to_all | solution.py:232
  30.3 3.0 %collective-permute-start = (f32[512,128]{1,0:T(8,128)S(1)}, f32[512,128]{1,0:T(8,128)S(1)}, u32[]{:S(2)}, u32[]{:S(2)}) collective-permute-start(f32[512,128]{1,0:T(8,128)S(1)} %bitcast.14), channel_id=1, source_target_pairs={{0,32},{32,0},{1,33},{33,1},{2,34},{34,2},{3,35},{35,3},{4,36},{36... | collective-permute-start | bytes 786440 | tf_op jit(solution)/shard_map/ppermute | solution.py:252
  33.4 1.6 %own.1 = (f32[512,128]{1,0:T(8,128)S(1)}, bf16[2048,128]{1,0:T(8,128)(2,1)S(1)}, bf16[112,2048]{1,0:T(8,128)(2,1)S(1)}, bf16[128,512]{1,0:T(8,128)(2,1)S(1)}, f3...) custom-call(f32[512,128]{1,0:T(8,128)S(1)} %bitcast.15), custom_call_target="tpu_custom_call" | custom-call | flops 2147483648 | bytes 1048576 | tf_op jit(solution)/shard_map/own/pallas_call | solution.py:264
  35.0 0.0 collective-permute-done.refs_0_
  35.0 3.8 %tile.1 = f32[256,128]{1,0:T(8,128)S(1)} custom-call(f32[512,128]{1,0:T(8,128)S(1)} %collective-permute-done.refs_0_, f32[512,128]{1,0:T(8,128)S(1)} %get-tuple-element.12.refs_1_, bf16[2048,128]{1,0:T(8,128)(2,1)S(1)} %get-tuple-element.13.refs_2_, bf16[112,2048]{1,0:T(8,128)(2,1)S(1)} %get-tuple-element.14.refs_3_, ...), custom_call_target="tpu_custom_call" | custom-call | tf_op jit(solution)/shard_map/tile/pallas_call | solution.py:273
  38.8 17.7 %all_to_all.11 = f32[256,1,128]{2,1,0:T(1,128)S(1)} all-to-all(f32[256,1,128]{2,1,0:T(1,128)S(1)} %bitcast.12), channel_id=1, replica_groups=mesh['row_0'=4,'row_1'=2,'col_0'=8,'col_1'=4] {'row_0','col_0','col_1','..., dimensions={0} | all-to-all | bytes 262144 | tf_op jit(solution)/shard_map/all_to_all | solution.py:232
  56.5 0.8 %finish.1 = (f32[16,128]{1,0:T(8,128)}, f32[1,128]{1,0:T(1,128)}, f32[1,16]{1,0:T(1,128)}) custom-call(f32[256,128]{1,0:T(8,128)S(1)} %bitcast.13), custom_call_target="tpu_custom_call" | custom-call | tf_op jit(solution)/shard_map/finish/pallas_call | solution.py:286
Async XLA Ops:
  30.3 4.7 %collective-permute-start = (f32[512,128]{1,0:T(8,128)S(1)}, f32[512,128]{1,0:T(8,128)S(1)}, u32[]{:S(2)}, u32[]{:S(2)}) collective-permute-start(f32[512,128]{1,0:T(8,128)S(1)} %bitcast.14), channel_id=1, source_target_pairs={{0,32},{32,0},{1,33},{33,1},{2,34},{34,2},{3,35},{35,3},{4,36},{36... | collective-permute-start | bytes 786440 | tf_op jit(solution)/shard_map/ppermute | solution.py:252

commit v8 on v7

--- a/solution.py
+++ b/solution.py
@@ -9,7 +9,7 @@
 from jax.sharding import PartitionSpec as P
 
 CORE = "row_1"
-CHIPS = ("row_0", "col_0", "col_1")
+CHIPS = ("col_1", "col_0", "row_0")
 CHIPS_CORE = (*CHIPS, CORE)
 ROW_COL = ("row_0", "row_1", "col_0", "col_1")
 COL_ROW = ("col_0", "col_1", "row_0", "row_1")

time: 57.5 us -> 57.5 us (level)
  no operation moved by 1% of the time
where the time goes in v8:
time: 57.5 us; the launch traced here: 57.3 us
  blocking collectives  46.3 us (81%)
  Pallas kernels  7.3 us (13%)
  starting transfers between devices  3.02 us (5%)
  between operations  0.66 us (1%)
    all_to_all x2, blocking collectives, exchanged(): lax.all_to_all(blocks, axes, split_axis=0, concat_axis=0, tiled=True)  46.3 us
    pallas_call x1, Pallas kernels, on_device(): pl.pallas_call(lambda *refs: tile_kernel(plan, *refs), out_shape=jax.Shap...  3.81 us
    ppermute x1, starting transfers between devices, on_device(): other = lax.ppermute(own, CORE, [(0, 1), (1, 0)])  3.02 us
    pallas_call x1, Pallas kernels, on_device(): pl.pallas_call(lambda *refs: own_kernel(plan, *refs), out_shape=prepared...  1.65 us
  transfers between devices with their start and end apart: 1, of which 0 were waited for; matrix products, arithmetic and copies ran while one was open for 0% of the time, Pallas kernels for 3%

profile of v8, /device:TPU:1, one launch (start us, length us, event | category | flops | bytes accessed | tf_op | source)
XLA Modules:
  0.0 57.3 jit_solution(5792482148823315084)
XLA Ops:
  0.6 1.1 %spread.1 = f32[512,128]{1,0:T(8,128)S(1)} custom-call(f32[16,128]{1,0:T(8,128)} %refs_0_.1, f32[1,128]{1,0:T(1,128)} %bitcast.16, f32[16,128]{1,0:T(8,128)} %refs_2_.1, f32[1,128]{1,0:T(1,128)} %bitcast.17, f32[1,16]{1,0:T(1,128)} %bitcast.18), custom_call_target="tpu_custom_call" | custom-call | tf_op jit(solution)/shard_map/spread/pallas_call | solution.py:235
  1.7 28.6 %all_to_all.10 = f32[128,1,512]{2,1,0:T(1,128)S(1)} all-to-all(f32[128,1,512]{2,1,0:T(1,128)S(1)} %bitcast.11), channel_id=1, replica_groups=mesh['row_0'=4,'row_1'=2,'col_0'=8,'col_1'=4] {'col_1','col_0','row_0'}, dimensions={0} | all-to-all | bytes 524288 | tf_op jit(solution)/shard_map/all_to_all | solution.py:232
  30.3 3.0 %collective-permute-start = (f32[512,128]{1,0:T(8,128)S(1)}, f32[512,128]{1,0:T(8,128)S(1)}, u32[]{:S(2)}, u32[]{:S(2)}) collective-permute-start(f32[512,128]{1,0:T(8,128)S(1)} %bitcast.14), channel_id=1, source_target_pairs={{0,32},{32,0},{1,33},{33,1},{2,34},{34,2},{3,35},{35,3},{4,36},{36... | collective-permute-start | bytes 786440 | tf_op jit(solution)/shard_map/ppermute | solution.py:252
  33.4 1.6 %own.1 = (f32[512,128]{1,0:T(8,128)S(1)}, bf16[2048,128]{1,0:T(8,128)(2,1)S(1)}, bf16[112,2048]{1,0:T(8,128)(2,1)S(1)}, bf16[128,512]{1,0:T(8,128)(2,1)S(1)}, f3...) custom-call(f32[512,128]{1,0:T(8,128)S(1)} %bitcast.15), custom_call_target="tpu_custom_call" | custom-call | flops 2147483648 | bytes 1048576 | tf_op jit(solution)/shard_map/own/pallas_call | solution.py:264
  35.0 0.0 collective-permute-done.refs_0_
  35.0 3.8 %tile.1 = f32[256,128]{1,0:T(8,128)S(1)} custom-call(f32[512,128]{1,0:T(8,128)S(1)} %collective-permute-done.refs_0_, f32[512,128]{1,0:T(8,128)S(1)} %get-tuple-element.12.refs_1_, bf16[2048,128]{1,0:T(8,128)(2,1)S(1)} %get-tuple-element.13.refs_2_, bf16[112,2048]{1,0:T(8,128)(2,1)S(1)} %get-tuple-element.14.refs_3_, ...), custom_call_target="tpu_custom_call" | custom-call | tf_op jit(solution)/shard_map/tile/pallas_call | solution.py:273
  38.8 17.7 %all_to_all.11 = f32[256,1,128]{2,1,0:T(1,128)S(1)} all-to-all(f32[256,1,128]{2,1,0:T(1,128)S(1)} %bitcast.12), channel_id=1, replica_groups=mesh['row_0'=4,'row_1'=2,'col_0'=8,'col_1'=4] {'col_1','col_0','row_0','..., dimensions={0} | all-to-all | bytes 262144 | tf_op jit(solution)/shard_map/all_to_all | solution.py:232
  56.5 0.8 %finish.1 = (f32[16,128]{1,0:T(8,128)}, f32[1,128]{1,0:T(1,128)}, f32[1,16]{1,0:T(1,128)}) custom-call(f32[256,128]{1,0:T(8,128)S(1)} %bitcast.13), custom_call_target="tpu_custom_call" | custom-call | tf_op jit(solution)/shard_map/finish/pallas_call | solution.py:286
Async XLA Ops:
  30.3 4.7 %collective-permute-start = (f32[512,128]{1,0:T(8,128)S(1)}, f32[512,128]{1,0:T(8,128)S(1)}, u32[]{:S(2)}, u32[]{:S(2)}) collective-permute-start(f32[512,128]{1,0:T(8,128)S(1)} %bitcast.14), channel_id=1, source_target_pairs={{0,32},{32,0},{1,33},{33,1},{2,34},{34,2},{3,35},{35,3},{4,36},{36... | collective-permute-start | bytes 786440 | tf_op jit(solution)/shard_map/ppermute | solution.py:252
